TPU v7x, 256 devices: a whole 4x4x8 slice. The times are simulated.
256 devices in a mesh: gx: 8 (over x, core), gy: 32 (over y, z).
Axes of the slice: x: 4, y: 4, z: 8, core: 2. Of those that a mesh axis runs over, the one named last changes fastest.
Arguments:
- features: bfloat16 [65536, 128], P(('gx', 'gy')), may hold values from -6 to 6
- tile_vals: bfloat16 [16384, 128, 128], P(('gx', 'gy')), may hold values from -0.125 to 0.125
- tile_row: int32 [16384], P(('gx', 'gy')), may hold values from 0 to 511, as said below
- tile_col: int32 [16384], P(('gx', 'gy')), may hold values from 0 to 511, as said below
- tile_work: int32 [16384], P(('gx', 'gy')), may hold values from 0 to 16384, as said below
Outputs:
- product: float32 [65536, 128], P(('gx', 'gy'))
- moved_vals: bfloat16 [8192, 128, 128], P(('gx', 'gy'))
- moved_row: int32 [8192], P(('gx', 'gy'))
- moved_col: int32 [8192], P(('gx', 'gy'))
- moved_work: int32 [8192], P(('gx', 'gy'))
Inputs may be any that keep to these rules, and one draw needn't show every extreme that they name: `tile_work`: on every device the live slots come first; each gx row of 32 devices holds exactly 1024 live tiles, and in every row one device has all 64 slots live. `tile_row`: A tile held by device (a, b) has a row block owned by a device of gx index a. `tile_col`: A tile held by device (a, b) has a column block owned by a device of gy index b.
All inputs are finite; a program needn't handle non-finite values.
Results may differ from a plain program's by a relative error of at most 0.001.
Values may be sent and summed in bfloat16 or wider, within the bound.
No kernel may reach another device: no remote copies, remote signals or barrier semaphores. Data moves between devices by JAX's collectives and lax.ppermute only.
A program may use at most 64 MiB of HBM per device.

v0:
```python
import jax
import jax.numpy as jnp
from jax import lax
from jax.experimental import pallas as pl
from jax.experimental.pallas import tpu as pltpu
from jax.sharding import Mesh
from jax.sharding import PartitionSpec as P

GY = ("y", "z")
GX_GY = ("gx", "y", "z")

ANY = pl.BlockSpec(memory_space=pl.ANY)
SMEM = pl.BlockSpec(memory_space=pltpu.SMEM)
VMEM = pl.BlockSpec(memory_space=pltpu.VMEM)


def in_vmem(array):
    return pltpu.with_memory_space_constraint(array, pltpu.VMEM)


def in_hbm(array):
    return pltpu.with_memory_space_constraint(array, pltpu.HBM)


def vmem(shape, dtype):
    return pltpu.VMEM(shape, dtype)


def limit(mib):
    return pltpu.CompilerParams(vmem_limit_bytes=mib * 2**20)


def shifted(array, axis, by):
    size = lax.axis_size(axis)
    return lax.ppermute(array, axis, [(i, (i + by) % size) for i in range(size)])


def tell_kernel(slots, row_ref, col_ref, work_ref, out_ref, held, sems):
    copies = [
        pltpu.make_async_copy(ref, held.at[i], sems.at[i]) for i, ref in enumerate((row_ref, col_ref, work_ref))
    ]
    for c in copies:
        c.start()
    for c in copies:
        c.wait()
    row, col, work = (held[i].reshape(1, slots) for i in range(3))
    count = jnp.sum((work > 0).astype(jnp.int32), axis=1, keepdims=True)
    for i, pair in enumerate(((row, col), (work, jnp.broadcast_to(count, (1, slots))))):
        line = jnp.concatenate(pair, axis=1)
        out_ref[:, i, :] = jnp.broadcast_to(line, (out_ref.shape[0], 2 * slots))


def stage_kernel(vals_ref, out_ref, sems):
    groups = sems.shape[0]
    size = vals_ref.shape[0] // groups
    copies = [
        pltpu.make_async_copy(
            vals_ref.at[pl.ds(g * size, size)], out_ref.at[pl.ds(g * size, size)], sems.at[g]
        )
        for g in range(groups)
    ]
    for c in copies:
        c.start()
    for c in copies:
        c.wait()


def place_of():
    return lax.axis_index("y") * lax.axis_size("z") + lax.axis_index("z")


def plan_kernel(peers, slots, meta_ref, vals_ref, sent_ref, sems):
    me = place_of()
    share = slots // peers

    counts = meta_ref[:, 1, :]
    earlier = (lax.broadcasted_iota(jnp.int32, counts.shape, 0) < me) & (
        lax.broadcasted_iota(jnp.int32, counts.shape, 1) == slots
    )
    first = jnp.sum(jnp.where(earlier, counts, 0).astype(jnp.float32)).astype(jnp.int32)
    turn = lax.rem(first, peers)

    def start(d, carry):
        at = lax.rem(d - turn + peers, peers)
        for w in range(share):
            pltpu.make_async_copy(
                vals_ref.at[at + w * peers], sent_ref.at[d * share + w], sems.at[0]
            ).start()
        return carry

    lax.fori_loop(0, peers, start, 0, unroll=8)
    pltpu.make_async_copy(vals_ref, sent_ref, sems.at[0]).wait()


def list_kernel(peers, slots, meta_ref, row_ref, col_ref, work_ref, slot_ref):
    me = place_of()
    share = slots // peers

    def source(s, begin):
        count = meta_ref[s, 1, slots]
        j = lax.rem(me - lax.rem(begin, peers) + peers, peers)
        for w in range(share):
            at = j + w * peers

            @pl.when(at < count)
            def _():
                k = lax.div(begin + at, peers)
                row_ref[k] = meta_ref[s, 0, at]
                col_ref[k] = meta_ref[s, 0, slots + at]
                work_ref[k] = meta_ref[s, 1, at]
                slot_ref[k] = s * share + w

        return begin + count

    lax.fori_loop(0, peers, source, jnp.int32(0))


def keep_kernel(owned, slot_ref, got_ref, out_ref, sems):
    def start(k, carry):
        pltpu.make_async_copy(got_ref.at[slot_ref[k]], out_ref.at[k], sems.at[0]).start()
        return carry

    lax.fori_loop(0, owned, start, 0)
    pltpu.make_async_copy(got_ref.at[pl.ds(0, owned)], out_ref, sems.at[0]).wait()


MARGIN = 0.999


def coded(x, q_ref, exps_ref, at, row):
    top = jnp.maximum(jnp.max(jnp.abs(x), axis=0, keepdims=True), 1e-30)
    exponent = jnp.ceil(jnp.log2(top))
    scaled = jnp.round(x * (jnp.exp2(15.0 - exponent) * MARGIN))
    q_ref[pl.ds(at, x.shape[0]), :] = scaled.astype(jnp.int32).astype(jnp.int16)
    exps_ref[pl.ds(row, 1), :] = exponent


def product_kernel(gx, gy, groups, steps, row_ref, col_ref, work_ref, tiles, *refs):
    feats, refs = refs[:gx], refs[gx:]
    keep_ref, even_ref, odd_ref, acc, held, made, exps, codes, sems = refs
    slots, order, _ = tiles.shape
    per_step = slots // steps
    vblocks = held.shape[0] // gx
    blocks = acc.shape[0]
    span = blocks // groups
    a = lax.axis_index("gx")
    cores = 2

    acc[...] = jnp.zeros_like(acc)
    for k, f in enumerate(feats):
        held[pl.ds(k * f.shape[0], f.shape[0])] = f[...]

    pattern = lax.broadcasted_iota(jnp.int32, (order, order), 0) * order + lax.broadcasted_iota(
        jnp.int32, (order, order), 1
    )
    for i in range(steps):

        def form(t, carry):
            tile = i * per_step + t
            col = col_ref[tile]
            home = lax.div(col, gy * vblocks)
            away = lax.rem(lax.div(a, cores) - lax.div(home, cores) + gx, gx // cores)
            side = lax.rem(a + home, cores)
            place = (side * (gx // cores) + away) * vblocks + lax.rem(col, vblocks)
            masked = jnp.where(pattern < work_ref[tile], tiles[tile], jnp.zeros((), jnp.bfloat16))
            made[t] = jnp.dot(masked, held[place], preferred_element_type=jnp.float32)
            return carry

        lax.fori_loop(0, per_step, form, 0, unroll=True)

        def add(t, carry):
            row = lax.rem(row_ref[i * per_step + t], blocks)
            acc[row] += made[t]
            return carry

        lax.fori_loop(0, per_step, add, 0, unroll=True)

    owners = span // vblocks
    pairs = owners // 2
    side = lax.rem(lax.axis_index("z"), 2)

    def leave(n, carry):
        at = lax.div(n, pairs) * span + (2 * lax.rem(n, pairs) + side) * vblocks
        pltpu.make_async_copy(
            acc.at[pl.ds(at, vblocks)], keep_ref.at[pl.ds(n * vblocks, vblocks)], sems.at[0]
        ).start()
        return carry

    lax.fori_loop(0, groups * pairs, leave, 0)
    lines = groups * pairs
    parts = 2
    leaving = []
    for v, q_ref in enumerate((even_ref, odd_ref)):
        held_codes = codes.at[v]

        def code(n, carry):
            at = lax.div(n, pairs) * span + (2 * lax.rem(n, pairs) + 1 - side) * vblocks + v
            coded(acc[at], held_codes, exps, n * order, n)
            return carry

        for i in range(parts):
            lax.fori_loop(i * lines // parts, (i + 1) * lines // parts, code, 0, unroll=2)
            if i == parts - 1:
                store_exps(held_codes, exps, lines, order)
            begin = i * lines * order // parts
            size = q_ref.shape[0] - begin if i == parts - 1 else lines * order // parts
            leaving.append(
                pltpu.make_async_copy(
                    held_codes.at[pl.ds(begin, size)], q_ref.at[pl.ds(begin, size)], sems.at[1 + v * parts + i]
                )
            )
            leaving[-1].start()
    for c in leaving:
        c.wait()
    pltpu.make_async_copy(acc.at[pl.ds(0, keep_ref.shape[0])], keep_ref, sems.at[0]).wait()


def scales_of(ref, at):
    exps = ref[pl.ds(at, ref.shape[0] - at), :].astype(jnp.int32).astype(jnp.float32)
    return jnp.exp2(exps - 15.0) * (1.0 / MARGIN)


def part_of(ref, i, order, count):
    x = ref[pl.ds(i * order, order), :].astype(jnp.int32).astype(jnp.float32)
    return x * scales_of(ref, count * order)[i : i + 1, :]


def store_exps(q_ref, exps, count, order):
    q_ref[pl.ds(count * order, exps.shape[0]), :] = exps[...].astype(jnp.int32).astype(jnp.int16)


def join_kernel(order, vblocks, groups, keep_ref, even_ref, odd_ref, own_ref, rest_ref, right_ref, left_ref, scales, exps):
    span = keep_ref.shape[0] // groups
    half = span // 2
    lines = groups * span // vblocks
    y = lax.axis_index("y")
    got = (even_ref, odd_ref)
    for v, g in enumerate(got):
        scales[pl.ds(v * lines, lines), :] = scales_of(g, lines * order)

    def total(chunk, pair, v):
        n = chunk * (span // vblocks) + pair
        x = got[v][pl.ds(n * order, order), :].astype(jnp.int32).astype(jnp.float32)
        return keep_ref[n * vblocks + v] + x * scales[pl.ds(v * lines + n, 1), :]

    there, far, behind = (lax.rem(y + k, groups) for k in range(1, groups))
    low, high = 0, half // vblocks
    for chunk, start, at in ((y, low, 0), (y, high, half)):
        for i in range(half // vblocks):
            for v in range(vblocks):
                own_ref[at + i * vblocks + v] = total(chunk, start + i, v)
    for chunk, start, at in ((there, low, 0), (behind, high, half)):
        for i in range(half // vblocks):
            for v in range(vblocks):
                rest_ref[at + i * vblocks + v] = total(chunk, start + i, v)
    for q_ref, parts in ((right_ref, ((far, low), (there, high))), (left_ref, ((far, high), (behind, low)))):
        for n, (chunk, start) in enumerate(parts):
            for i in range(half // vblocks):
                for v in range(vblocks):
                    row = n * half + i * vblocks + v
                    coded(total(chunk, start + i, v), q_ref, exps, row * order, row)
        store_exps(q_ref, exps, span, order)


def relay_kernel(order, rest_ref, low_ref, high_ref, right_ref, left_ref, scales, exps):
    span = rest_ref.shape[0]
    half = span // 2
    exps[...] = jnp.zeros_like(exps)
    for side, (got, q_ref) in enumerate(((low_ref, right_ref), (high_ref, left_ref))):
        scales[...] = scales_of(got, span * order)
        for i in range(half):
            part = got[pl.ds(i * order, order), :].astype(jnp.int32).astype(jnp.float32)
            x = rest_ref[side * half + i] + part * scales[pl.ds(i, 1), :]
            coded(x, q_ref, exps, i * order, i)
        store_exps(q_ref, exps, half, order)


def middle_kernel(order, vblocks, own_ref, low_ref, high_ref, low2_ref, high2_ref, out_ref, *refs):
    q_refs, (total, exps) = refs[:-2], refs[-2:]
    span = own_ref.shape[0]
    half = span // 2
    owners = span // vblocks
    mine = lax.div(lax.axis_index("z"), 2)
    exps[...] = jnp.zeros_like(exps)
    for side, (near, last) in enumerate(((high_ref, low2_ref), (low_ref, high2_ref))):
        near_scales, last_scales = scales_of(near, span * order), scales_of(last, half * order)
        for i in range(half):
            x = own_ref[side * half + i]
            for ref, at, scale in ((near, half + i, near_scales[half + i : half + i + 1]), (last, i, last_scales[i : i + 1])):
                x = x + ref[pl.ds(at * order, order), :].astype(jnp.int32).astype(jnp.float32) * scale
            total[side * half + i] = x
    for v in range(vblocks):
        out_ref[pl.ds(v * order, order), :] = total[mine * vblocks + v]
    for k, q_ref in enumerate(q_refs, 1):
        base = lax.rem(mine + k, owners) * vblocks
        for v in range(vblocks):
            coded(total[base + v], q_ref, exps, v * order, v)
        store_exps(q_ref, exps, vblocks, order)


def last_kernel(order, vblocks, own_ref, *refs):
    got, out_ref = refs[:-1], refs[-1]
    for v in range(vblocks):
        x = own_ref[pl.ds(v * order, order), :]
        for g in got:
            x = x + part_of(g, v, order, vblocks)
        out_ref[pl.ds(v * order, order), :] = x


def on_device(features, tile_vals, tile_row, tile_col, tile_work):
    peers = lax.axis_size(GY)
    gx, ny, nz = (lax.axis_size(axis) for axis in GX_GY)
    slots, order, _ = tile_vals.shape
    owned = slots // 2
    width = features.shape[1]
    vblocks = features.shape[0] // order
    blocks = peers * vblocks
    told = pl.pallas_call(
        lambda *refs: tell_kernel(slots, *refs),
        in_specs=[ANY] * 3,
        out_specs=VMEM,
        out_shape=jax.ShapeDtypeStruct((peers, 2, 2 * slots), jnp.int32),
        scratch_shapes=[pltpu.VMEM((3, slots), jnp.int32), pltpu.SemaphoreType.DMA((3,))],
        compiler_params=limit(4),
        name="tell",
    )(*(in_hbm(t) for t in (tile_row, tile_col, tile_work)))

    cores = 2
    mine = [features.reshape(vblocks, order, width)]
    for k in range(1, gx // cores):
        mine.append(lax.ppermute(mine[0], "gx", [(i, (i + cores * k) % gx) for i in range(gx)]))
    meta = lax.all_to_all(told, GY, split_axis=0, concat_axis=0, tiled=True)
    swapped = []
    for f in mine:
        swapped.append(lax.ppermute(f, "gx", [(i, i ^ 1) for i in range(gx)]))
    tiles = pl.pallas_call(
        stage_kernel,
        in_specs=[ANY],
        out_specs=VMEM,
        out_shape=vmem(tile_vals.shape, tile_vals.dtype),
        scratch_shapes=[pltpu.SemaphoreType.DMA((8,))],
        compiler_params=limit(4),
        name="stage",
    )(in_hbm(tile_vals))
    small = jax.ShapeDtypeStruct((owned,), jnp.int32)
    sent = pl.pallas_call(
        lambda *refs: plan_kernel(peers, slots, *refs),
        in_specs=[VMEM, VMEM],
        out_specs=ANY,
        out_shape=pltpu.HBM(tile_vals.shape, tile_vals.dtype),
        scratch_shapes=[pltpu.SemaphoreType.DMA((1,))],
        compiler_params=limit(4),
        name="plan",
    )(in_vmem(meta), in_vmem(tiles))
    moved_row, moved_col, moved_work, kept = pl.pallas_call(
        lambda *refs: list_kernel(peers, slots, *refs),
        in_specs=[SMEM],
        out_specs=[SMEM] * 4,
        out_shape=[small] * 4,
        compiler_params=limit(4),
        name="list",
    )(meta)
    got = lax.all_to_all(sent, GY, split_axis=0, concat_axis=0, tiled=True)

    steps = 8
    span = blocks // ny
    i16 = jnp.int16

    def line(count, more=8):
        return vmem((count * order + more, width), i16)

    lines = blocks // 2 // vblocks
    few = span // 2
    keep, even, odd = pl.pallas_call(
        lambda *refs: product_kernel(gx, peers, ny, steps, *refs),
        in_specs=[SMEM] * 3 + [VMEM] * (1 + gx),
        out_specs=[ANY] * 3,
        out_shape=[pltpu.HBM((blocks // 2, order, width), jnp.float32)]
        + [pltpu.HBM((lines * order + lines, width), i16)] * 2,
        scratch_shapes=[
            pltpu.VMEM((blocks, order, width), jnp.float32),
            pltpu.VMEM((gx * vblocks, order, width), jnp.bfloat16),
            pltpu.VMEM((slots // steps, order, width), jnp.float32),
            pltpu.VMEM((lines, width), jnp.float32),
            pltpu.VMEM((2, lines * order + lines, width), i16),
            pltpu.SemaphoreType.DMA((5,)),
        ],
        compiler_params=limit(16),
        name="products",
    )(tile_row, tile_col, tile_work, *(in_vmem(f) for f in (tiles, *mine, *swapped)))
    near = []
    for v, q in enumerate((even, odd)):
        near.append(lax.ppermute(q, "z", [(i, ((i + v) ^ 1) - v & nz - 1) for i in range(nz)]))
    some = vmem((few, order, width), jnp.float32)
    own, rest, right, left = pl.pallas_call(
        lambda *refs: join_kernel(order, vblocks, ny, *refs),
        in_specs=[VMEM] * 3,
        out_specs=[VMEM] * 4,
        out_shape=[some, some, line(few), line(few)],
        scratch_shapes=[pltpu.VMEM((2 * lines, width), jnp.float32), pltpu.VMEM((8, width), jnp.float32)],
        compiler_params=limit(12),
        name="join",
    )(keep, *near)
    low, high = shifted(right, "y", 1), shifted(left, "y", -1)
    right, left = pl.pallas_call(
        lambda *refs: relay_kernel(order, *refs),
        in_specs=[VMEM] * 3,
        out_specs=[VMEM] * 2,
        out_shape=[line(few // 2)] * 2,
        scratch_shapes=[pltpu.VMEM((8, width), jnp.float32), pltpu.VMEM((8, width), jnp.float32)],
        compiler_params=limit(8),
        name="relay",
    )(rest, low, high)
    low2, high2 = shifted(right, "y", 1), shifted(left, "y", -1)
    own_z, *coded_z = pl.pallas_call(
        lambda *refs: middle_kernel(order, vblocks, *refs),
        in_specs=[VMEM] * 5,
        out_specs=[VMEM] * (nz // 2),
        out_shape=[vmem((vblocks * order, width), jnp.float32)] + [line(vblocks)] * (nz // 2 - 1),
        scratch_shapes=[pltpu.VMEM((few, order, width), jnp.float32), pltpu.VMEM((8, width), jnp.float32)],
        compiler_params=limit(8),
        name="middle",
    )(own, low, high, low2, high2)
    got_z = []
    for k, q in enumerate(coded_z, 1):
        got_z.append(shifted(q, "z", 2 * k))
    product = pl.pallas_call(
        lambda *refs: last_kernel(order, vblocks, *refs),
        in_specs=[VMEM] * (nz // 2),
        out_specs=VMEM,
        out_shape=jax.ShapeDtypeStruct((vblocks * order, width), jnp.float32),
        compiler_params=limit(4),
        name="last",
    )(*(in_vmem(g) for g in (own_z, *got_z)))

    moved_vals = pl.pallas_call(
        lambda *refs: keep_kernel(owned, *refs),
        in_specs=[SMEM, VMEM],
        out_specs=ANY,
        out_shape=jax.ShapeDtypeStruct((owned, *tile_vals.shape[1:]), tile_vals.dtype),
        scratch_shapes=[pltpu.SemaphoreType.DMA((1,))],
        compiler_params=limit(4),
        name="keep",
    )(kept, in_vmem(got))
    return (product, moved_vals, moved_row, moved_col, moved_work)


def solution(mesh):
    finer = Mesh(mesh.devices.reshape(mesh.shape["gx"], 4, 8), GX_GY)
    in_specs = (P(GX_GY, None), P(GX_GY, None, None), P(GX_GY), P(GX_GY), P(GX_GY))

    return jax.shard_map(on_device, mesh=finer, in_specs=in_specs, out_specs=in_specs, check_vma=False)
```

profile of v0, /device:TPU:40, one launch (start us, length us, event | category | flops | bytes accessed | tf_op | source)
XLA Modules:
  0.0 119.3 jit_solution(9030582654615706944)
XLA Ops:
  0.6 1.4 %tell.1 = s32[32,2,128]{2,1,0:T(2,128)} custom-call(s32[64]{0:T(128)} %refs_0_.3, s32[64]{0:T(128)} %refs_1_.3, s32[64]{0:T(128)} %refs_2_.3), custom_call_target="tpu_custom_call" | custom-call | tf_op jit(solution)/shard_map/tell/pallas_call | solution.py:318
  2.1 11.3 %all-to-all-start = ((s32[32,2,128]{2,1,0:T(2,128)}), s32[32,2,128]{2,1,0:T(2,128)S(1)}, u32[]{:S(2)}, u32[]{:S(2)}) async-start(s32[32,2,128]{2,1,0:T(2,128)} %tell.1), calls=%async_computation | async-start | bytes 65536 | tf_op jit(solution)/shard_map/all_to_all | solution.py:332
  13.3 1.6 %stage.1.refs_3_.refs_1_ = bf16[64,128,128]{2,1,0:T(8,128)(2,1)S(1)} custom-call(bf16[64,128,128]{2,1,0:T(8,128)(2,1)} %vals_ref.1), custom_call_target="tpu_custom_call" | custom-call | tf_op jit(solution)/shard_map/stage/pallas_call | solution.py:336
  14.9 6.4 %all-to-all-done.refs_0_ = s32[32,2,128]{2,1,0:T(2,128)S(1)} async-done(((s32[32,2,128]{2,1,0:T(2,128)}), s32[32,2,128]{2,1,0:T(2,128)S(1)}, u32[]{:S(2)}, u32[]{:S(2)}) %all-to-all-start) | async-done | bytes 32800 | tf_op jit(solution)/shard_map/all_to_all | solution.py:332
  21.3 1.5 %plan.1 = bf16[64,128,128]{2,1,0:T(8,128)(2,1)} custom-call(s32[32,2,128]{2,1,0:T(2,128)S(1)} %all-to-all-done.refs_0_, bf16[64,128,128]{2,1,0:T(8,128)(2,1)S(1)} %stage.1.refs_3_.refs_1_), custom_call_target="tpu_custom_call" | custom-call | tf_op jit(solution)/shard_map/plan/pallas_call | solution.py:346
  22.8 6.7 %all-to-all-start.1 = ((bf16[64,128,128]{2,1,0:T(8,128)(2,1)}), bf16[64,128,128]{2,1,0:T(8,128)(2,1)}, u32[]{:S(2)}, u32[]{:S(2)}) async-start(bf16[64,128,128]{2,1,0:T(8,128)(2,1)} %plan.1), calls=%async_computation.1 | async-start | bytes 4194304 | tf_op jit(solution)/shard_map/all_to_all | solution.py:363
  29.5 2.8 %collective-permute-start.2 = (bf16[2,128,128]{2,1,0:T(8,128)(2,1)S(1)}, bf16[2,128,128]{2,1,0:T(8,128)(2,1)S(1)}, u32[]{:S(2)}, u32[]{:S(2)}) collective-permute-start(bf16[2,128,128]{2,1,0:T(8,128)(2,1)S(1)} %bitcast.1), channel_id=1, source_target_pairs={{0,192},{32,224},{64,0},{96,32},{128,64},{160,96},{192,128},{224,1... | collective-permute-start | bytes 196616 | tf_op jit(solution)/shard_map/ppermute | solution.py:331
  32.4 0.8 collective-permute-start.1
  33.2 0.9 collective-permute-start
  34.6 3.6 %collective-permute-done.1.refs_6_ = bf16[2,128,128]{2,1,0:T(8,128)(2,1)S(1)} collective-permute-done((bf16[2,128,128]{2,1,0:T(8,128)(2,1)S(1)}, bf16[2,128,128]{2,1,0:T(8,128)(2,1)S(1)}, u32[]{:S(2)}, u32[]{:S(2)}) %collective-permute-start.1) | collective-permute-done | bytes 65568 | tf_op jit(solution)/shard_map/ppermute | solution.py:331
  38.2 0.7 collective-permute-done.refs_5_
  38.9 0.6 collective-permute-done.5.refs_10_
  39.4 0.7 collective-permute-done.4.refs_9_
  40.1 3.6 %products.1 = (f32[32,128,128]{2,1,0:T(8,128)}, s16[2064,128]{1,0:T(8,128)(2,1)}, s16[2064,128]{1,0:T(8,128)(2,1)}) custom-call(s32[64]{0:T(128)S(1)} %copy-done.2, s32[64]{0:T(128)S(1)} %copy-done.3, s32[64]{0:T(128)S(1)} %copy-done.4, bf16[64,128,128]{2,1,0:T(8,128)(2,1)S(1)} %stage.1.refs_3_.refs_1_, bf16[2,128,128]{2,1,0:T(8,128)(2,1)S(1)} %bitcast.5, ...), custom_call_target="tpu_custom_call" | custom-call | tf_op jit(solution)/shard_map/products/pallas_call | solution.py:374
  43.7 0.6 collective-permute-start.7
  44.4 2.4 %collective-permute-start.8 = (s16[2064,128]{1,0:T(8,128)(2,1)}, s16[2064,128]{1,0:T(8,128)(2,1)S(1)}, u32[]{:S(2)}, u32[]{:S(2)}) collective-permute-start(s16[2064,128]{1,0:T(8,128)(2,1)} %get-tuple-element.24), channel_id=1, source_target_pairs={{0,7},{1,2},{2,1},{3,4},{4,3},{5,6},{6,5},{7,0},{8,15},{9,10},{10,... | collective-permute-start | bytes 1585160 | tf_op jit(solution)/shard_map/ppermute | solution.py:393
  46.8 38.6 %collective-permute-done.7.refs_1_ = s16[2064,128]{1,0:T(8,128)(2,1)S(1)} collective-permute-done((s16[2064,128]{1,0:T(8,128)(2,1)}, s16[2064,128]{1,0:T(8,128)(2,1)S(1)}, u32[]{:S(2)}, u32[]{:S(2)}) %collective-permute-start.7) | collective-permute-done | bytes 528416 | tf_op jit(solution)/shard_map/ppermute | solution.py:393
  85.4 1.0 collective-permute-done.8.refs_2_
  86.4 1.6 %copy-done = f32[32,128,128]{2,1,0:T(8,128)S(1)} copy-done((f32[32,128,128]{2,1,0:T(8,128)S(1)}, f32[32,128,128]{2,1,0:T(8,128)}, u32[]{:S(2)}) %copy-start) | copy-done | bytes 2097176
  88.4 1.6 %collective-permute-start.9 = (s16[1032,128]{1,0:T(8,128)(2,1)S(1)}, s16[1032,128]{1,0:T(8,128)(2,1)S(1)}, u32[]{:S(2)}, u32[]{:S(2)}) collective-permute-start(s16[1032,128]{1,0:T(8,128)(2,1)S(1)} %get-tuple-element.26), channel_id=1, source_target_pairs={{0,8},{8,16},{16,24},{24,0},{1,9},{9,17},{17,25},{25,1},{2,10},{10... | collective-permute-start | bytes 792584 | tf_op jit(solution)/shard_map/ppermute | solution.py:35
  90.5 5.3 %collective-permute-done.9.refs_1_ = s16[1032,128]{1,0:T(8,128)(2,1)S(1)} collective-permute-done((s16[1032,128]{1,0:T(8,128)(2,1)S(1)}, s16[1032,128]{1,0:T(8,128)(2,1)S(1)}, u32[]{:S(2)}, u32[]{:S(2)}) %collective-permute-start.9) | collective-permute-done | bytes 264224 | tf_op jit(solution)/shard_map/ppermute | solution.py:35
  95.9 1.2 %collective-permute-done.10.refs_2_ = s16[1032,128]{1,0:T(8,128)(2,1)S(1)} collective-permute-done((s16[1032,128]{1,0:T(8,128)(2,1)S(1)}, s16[1032,128]{1,0:T(8,128)(2,1)S(1)}, u32[]{:S(2)}, u32[]{:S(2)}) %collective-permute-start.10) | collective-permute-done | bytes 264224 | tf_op jit(solution)/shard_map/ppermute | solution.py:35
  97.3 1.3 %collective-permute-start.11 = (s16[520,128]{1,0:T(8,128)(2,1)S(1)}, s16[520,128]{1,0:T(8,128)(2,1)S(1)}, u32[]{:S(2)}, u32[]{:S(2)}) collective-permute-start(s16[520,128]{1,0:T(8,128)(2,1)S(1)} %get-tuple-element.29), channel_id=1, source_target_pairs={{0,8},{8,16},{16,24},{24,0},{1,9},{9,17},{17,25},{25,1},{2,10},{10... | collective-permute-start | bytes 399368 | tf_op jit(solution)/shard_map/ppermute | solution.py:35
  98.6 0.8 collective-permute-start.12
  99.4 3.0 %collective-permute-done.11.refs_3_ = s16[520,128]{1,0:T(8,128)(2,1)S(1)} collective-permute-done((s16[520,128]{1,0:T(8,128)(2,1)S(1)}, s16[520,128]{1,0:T(8,128)(2,1)S(1)}, u32[]{:S(2)}, u32[]{:S(2)}) %collective-permute-start.11) | collective-permute-done | bytes 133152 | tf_op jit(solution)/shard_map/ppermute | solution.py:35
  102.4 1.2 %collective-permute-done.12.refs_4_ = s16[520,128]{1,0:T(8,128)(2,1)S(1)} collective-permute-done((s16[520,128]{1,0:T(8,128)(2,1)S(1)}, s16[520,128]{1,0:T(8,128)(2,1)S(1)}, u32[]{:S(2)}, u32[]{:S(2)}) %collective-permute-start.12) | collective-permute-done | bytes 133152 | tf_op jit(solution)/shard_map/ppermute | solution.py:35
  103.8 3.5 %collective-permute-start.13 = (s16[264,128]{1,0:T(8,128)(2,1)S(1)}, s16[264,128]{1,0:T(8,128)(2,1)S(1)}, u32[]{:S(2)}, u32[]{:S(2)}) collective-permute-start(s16[264,128]{1,0:T(8,128)(2,1)S(1)} %get-tuple-element.32), channel_id=1, source_target_pairs={{0,2},{1,3},{2,4},{3,5},{4,6},{5,7},{6,0},{7,1},{8,10},{9,11},{10,... | collective-permute-start | bytes 202760 | tf_op jit(solution)/shard_map/ppermute | solution.py:35
  107.3 1.2 %collective-permute-start.14 = (s16[264,128]{1,0:T(8,128)(2,1)S(1)}, s16[264,128]{1,0:T(8,128)(2,1)S(1)}, u32[]{:S(2)}, u32[]{:S(2)}) collective-permute-start(s16[264,128]{1,0:T(8,128)(2,1)S(1)} %get-tuple-element.33), channel_id=1, source_target_pairs={{0,4},{1,5},{2,6},{3,7},{4,0},{5,1},{6,2},{7,3},{8,12},{9,13},{10,... | collective-permute-start | bytes 202760 | tf_op jit(solution)/shard_map/ppermute | solution.py:35
  108.5 4.0 %collective-permute-start.15 = (s16[264,128]{1,0:T(8,128)(2,1)S(1)}, s16[264,128]{1,0:T(8,128)(2,1)S(1)}, u32[]{:S(2)}, u32[]{:S(2)}) collective-permute-start(s16[264,128]{1,0:T(8,128)(2,1)S(1)} %get-tuple-element.34), channel_id=1, source_target_pairs={{0,6},{1,7},{2,0},{3,1},{4,2},{5,3},{6,4},{7,5},{8,14},{9,15},{10,... | collective-permute-start | bytes 202760 | tf_op jit(solution)/shard_map/ppermute | solution.py:35
  112.6 2.8 %list.1 = (s32[32]{0:T(128)}, s32[32]{0:T(128)}, s32[32]{0:T(128)}, s32[32]{0:T(128)S(1)}) custom-call(s32[32,2,128]{2,1,0:T(2,128)S(1)} %all-to-all-done.refs_0_), custom_call_target="tpu_custom_call" | custom-call | tf_op jit(solution)/shard_map/list/pallas_call | solution.py:355
  115.9 0.7 last.1
  116.6 2.6 %keep.1 = bf16[32,128,128]{2,1,0:T(8,128)(2,1)} custom-call(s32[32]{0:T(128)S(1)} %get-tuple-element.35.refs_0_, bf16[64,128,128]{2,1,0:T(8,128)(2,1)} %all-to-all-done.1.refs_1_), custom_call_target="tpu_custom_call" | custom-call | tf_op jit(solution)/shard_map/keep/pallas_call | solution.py:436
  (24 shorter events, 2.5 us)
Async XLA Ops:
  2.1 19.2 %all-to-all-start = ((s32[32,2,128]{2,1,0:T(2,128)}), s32[32,2,128]{2,1,0:T(2,128)S(1)}, u32[]{:S(2)}, u32[]{:S(2)}) async-start(s32[32,2,128]{2,1,0:T(2,128)} %tell.1), calls=%async_computation | async-start | bytes 65536 | tf_op jit(solution)/shard_map/all_to_all | solution.py:332
  22.8 6.8 %copy-start.1 = (bf16[256,128]{1,0:T(8,128)(2,1)S(1)}, bf16[256,128]{1,0:T(8,128)(2,1)}, u32[]{:S(2)}) copy-start(bf16[256,128]{1,0:T(8,128)(2,1)} %param.5) | copy-start | bytes 196612
  22.8 17.3 %copy-start.2 = (s32[64]{0:T(128)S(1)}, s32[64]{0:T(128)}, u32[]{:S(2)}) copy-start(s32[64]{0:T(128)} %refs_0_.3) | copy-start | bytes 772
  22.8 17.3 %copy-start.3 = (s32[64]{0:T(128)S(1)}, s32[64]{0:T(128)}, u32[]{:S(2)}) copy-start(s32[64]{0:T(128)} %refs_1_.3) | copy-start | bytes 772
  22.8 17.3 %copy-start.4 = (s32[64]{0:T(128)S(1)}, s32[64]{0:T(128)}, u32[]{:S(2)}) copy-start(s32[64]{0:T(128)} %refs_2_.3) | copy-start | bytes 772
  22.8 93.8 %all-to-all-start.1 = ((bf16[64,128,128]{2,1,0:T(8,128)(2,1)}), bf16[64,128,128]{2,1,0:T(8,128)(2,1)}, u32[]{:S(2)}, u32[]{:S(2)}) async-start(bf16[64,128,128]{2,1,0:T(8,128)(2,1)} %plan.1), calls=%async_computation.1 | async-start | bytes 4194304 | tf_op jit(solution)/shard_map/all_to_all | solution.py:363
  29.5 4.7 %collective-permute-start.2 = (bf16[2,128,128]{2,1,0:T(8,128)(2,1)S(1)}, bf16[2,128,128]{2,1,0:T(8,128)(2,1)S(1)}, u32[]{:S(2)}, u32[]{:S(2)}) collective-permute-start(bf16[2,128,128]{2,1,0:T(8,128)(2,1)S(1)} %bitcast.1), channel_id=1, source_target_pairs={{0,192},{32,224},{64,0},{96,32},{128,64},{160,96},{192,128},{224,1... | collective-permute-start | bytes 196616 | tf_op jit(solution)/shard_map/ppermute | solution.py:331
  32.4 5.8 %collective-permute-start.1 = (bf16[2,128,128]{2,1,0:T(8,128)(2,1)S(1)}, bf16[2,128,128]{2,1,0:T(8,128)(2,1)S(1)}, u32[]{:S(2)}, u32[]{:S(2)}) collective-permute-start(bf16[2,128,128]{2,1,0:T(8,128)(2,1)S(1)} %bitcast.2), channel_id=1, source_target_pairs={{0,128},{32,160},{64,192},{96,224},{128,0},{160,32},{192,64},{224,... | collective-permute-start | bytes 196616 | tf_op jit(solution)/shard_map/ppermute | solution.py:331
  33.2 5.7 %collective-permute-start = (bf16[2,128,128]{2,1,0:T(8,128)(2,1)S(1)}, bf16[2,128,128]{2,1,0:T(8,128)(2,1)S(1)}, u32[]{:S(2)}, u32[]{:S(2)}) collective-permute-start(bf16[2,128,128]{2,1,0:T(8,128)(2,1)S(1)} %bitcast.3), channel_id=1, source_target_pairs={{0,64},{32,96},{64,128},{96,160},{128,192},{160,224},{192,0},{224,... | collective-permute-start | bytes 196616 | tf_op jit(solution)/shard_map/ppermute | solution.py:331
  34.1 4.8 %collective-permute-start.3 = (bf16[2,128,128]{2,1,0:T(8,128)(2,1)S(1)}, bf16[2,128,128]{2,1,0:T(8,128)(2,1)S(1)}, u32[]{:S(2)}, u32[]{:S(2)}) collective-permute-start(bf16[2,128,128]{2,1,0:T(8,128)(2,1)S(1)} %bitcast.4), channel_id=1, source_target_pairs={{0,32},{32,0},{64,96},{96,64},{128,160},{160,128},{192,224},{224,1... | collective-permute-start | bytes 196616 | tf_op jit(solution)/shard_map/ppermute | solution.py:335
  34.3 4.6 %collective-permute-start.6 = (bf16[2,128,128]{2,1,0:T(8,128)(2,1)S(1)}, bf16[2,128,128]{2,1,0:T(8,128)(2,1)S(1)}, u32[]{:S(2)}, u32[]{:S(2)}) collective-permute-start(bf16[2,128,128]{2,1,0:T(8,128)(2,1)S(1)} %collective-permute-done.2.refs_7_), channel_id=1, source_target_pairs={{0,32},{32,0},{64,96},{96,64},{128,160},{160,128},{192,224},{224,1... | collective-permute-start | bytes 196616 | tf_op jit(solution)/shard_map/ppermute | solution.py:335
  38.2 1.3 %collective-permute-start.5 = (bf16[2,128,128]{2,1,0:T(8,128)(2,1)S(1)}, bf16[2,128,128]{2,1,0:T(8,128)(2,1)S(1)}, u32[]{:S(2)}, u32[]{:S(2)}) collective-permute-start(bf16[2,128,128]{2,1,0:T(8,128)(2,1)S(1)} %collective-permute-done.1.refs_6_), channel_id=1, source_target_pairs={{0,32},{32,0},{64,96},{96,64},{128,160},{160,128},{192,224},{224,1... | collective-permute-start | bytes 196616 | tf_op jit(solution)/shard_map/ppermute | solution.py:335
  38.9 1.3 %collective-permute-start.4 = (bf16[2,128,128]{2,1,0:T(8,128)(2,1)S(1)}, bf16[2,128,128]{2,1,0:T(8,128)(2,1)S(1)}, u32[]{:S(2)}, u32[]{:S(2)}) collective-permute-start(bf16[2,128,128]{2,1,0:T(8,128)(2,1)S(1)} %collective-permute-done.refs_5_), channel_id=1, source_target_pairs={{0,32},{32,0},{64,96},{96,64},{128,160},{160,128},{192,224},{224,1... | collective-permute-start | bytes 196616 | tf_op jit(solution)/shard_map/ppermute | solution.py:335
  43.7 41.7 %collective-permute-start.7 = (s16[2064,128]{1,0:T(8,128)(2,1)}, s16[2064,128]{1,0:T(8,128)(2,1)S(1)}, u32[]{:S(2)}, u32[]{:S(2)}) collective-permute-start(s16[2064,128]{1,0:T(8,128)(2,1)} %get-tuple-element.23), channel_id=1, source_target_pairs={{0,1},{1,0},{2,3},{3,2},{4,5},{5,4},{6,7},{7,6},{8,9},{9,8},{10,11... | collective-permute-start | bytes 1585160 | tf_op jit(solution)/shard_map/ppermute | solution.py:393
  44.4 42.0 %collective-permute-start.8 = (s16[2064,128]{1,0:T(8,128)(2,1)}, s16[2064,128]{1,0:T(8,128)(2,1)S(1)}, u32[]{:S(2)}, u32[]{:S(2)}) collective-permute-start(s16[2064,128]{1,0:T(8,128)(2,1)} %get-tuple-element.24), channel_id=1, source_target_pairs={{0,7},{1,2},{2,1},{3,4},{4,3},{5,6},{6,5},{7,0},{8,15},{9,10},{10,... | collective-permute-start | bytes 1585160 | tf_op jit(solution)/shard_map/ppermute | solution.py:393
  86.4 1.6 %copy-start = (f32[32,128,128]{2,1,0:T(8,128)S(1)}, f32[32,128,128]{2,1,0:T(8,128)}, u32[]{:S(2)}) copy-start(f32[32,128,128]{2,1,0:T(8,128)} %get-tuple-element.22.refs_0_) | copy-start | bytes 6291460
  88.4 7.4 %collective-permute-start.9 = (s16[1032,128]{1,0:T(8,128)(2,1)S(1)}, s16[1032,128]{1,0:T(8,128)(2,1)S(1)}, u32[]{:S(2)}, u32[]{:S(2)}) collective-permute-start(s16[1032,128]{1,0:T(8,128)(2,1)S(1)} %get-tuple-element.26), channel_id=1, source_target_pairs={{0,8},{8,16},{16,24},{24,0},{1,9},{9,17},{17,25},{25,1},{2,10},{10... | collective-permute-start | bytes 792584 | tf_op jit(solution)/shard_map/ppermute | solution.py:35
  90.0 7.1 %collective-permute-start.10 = (s16[1032,128]{1,0:T(8,128)(2,1)S(1)}, s16[1032,128]{1,0:T(8,128)(2,1)S(1)}, u32[]{:S(2)}, u32[]{:S(2)}) collective-permute-start(s16[1032,128]{1,0:T(8,128)(2,1)S(1)} %get-tuple-element.27), channel_id=1, source_target_pairs={{0,24},{8,0},{16,8},{24,16},{1,25},{9,1},{17,9},{25,17},{2,26},{10... | collective-permute-start | bytes 792584 | tf_op jit(solution)/shard_map/ppermute | solution.py:35
  97.3 5.1 %collective-permute-start.11 = (s16[520,128]{1,0:T(8,128)(2,1)S(1)}, s16[520,128]{1,0:T(8,128)(2,1)S(1)}, u32[]{:S(2)}, u32[]{:S(2)}) collective-permute-start(s16[520,128]{1,0:T(8,128)(2,1)S(1)} %get-tuple-element.29), channel_id=1, source_target_pairs={{0,8},{8,16},{16,24},{24,0},{1,9},{9,17},{17,25},{25,1},{2,10},{10... | collective-permute-start | bytes 399368 | tf_op jit(solution)/shard_map/ppermute | solution.py:35
  98.6 5.0 %collective-permute-start.12 = (s16[520,128]{1,0:T(8,128)(2,1)S(1)}, s16[520,128]{1,0:T(8,128)(2,1)S(1)}, u32[]{:S(2)}, u32[]{:S(2)}) collective-permute-start(s16[520,128]{1,0:T(8,128)(2,1)S(1)} %get-tuple-element.30), channel_id=1, source_target_pairs={{0,24},{8,0},{16,8},{24,16},{1,25},{9,1},{17,9},{25,17},{2,26},{10... | collective-permute-start | bytes 399368 | tf_op jit(solution)/shard_map/ppermute | solution.py:35
  103.8 11.5 %collective-permute-start.13 = (s16[264,128]{1,0:T(8,128)(2,1)S(1)}, s16[264,128]{1,0:T(8,128)(2,1)S(1)}, u32[]{:S(2)}, u32[]{:S(2)}) collective-permute-start(s16[264,128]{1,0:T(8,128)(2,1)S(1)} %get-tuple-element.32), channel_id=1, source_target_pairs={{0,2},{1,3},{2,4},{3,5},{4,6},{5,7},{6,0},{7,1},{8,10},{9,11},{10,... | collective-permute-start | bytes 202760 | tf_op jit(solution)/shard_map/ppermute | solution.py:35
  107.3 8.6 %collective-permute-start.14 = (s16[264,128]{1,0:T(8,128)(2,1)S(1)}, s16[264,128]{1,0:T(8,128)(2,1)S(1)}, u32[]{:S(2)}, u32[]{:S(2)}) collective-permute-start(s16[264,128]{1,0:T(8,128)(2,1)S(1)} %get-tuple-element.33), channel_id=1, source_target_pairs={{0,4},{1,5},{2,6},{3,7},{4,0},{5,1},{6,2},{7,3},{8,12},{9,13},{10,... | collective-permute-start | bytes 202760 | tf_op jit(solution)/shard_map/ppermute | solution.py:35
  108.5 7.4 %collective-permute-start.15 = (s16[264,128]{1,0:T(8,128)(2,1)S(1)}, s16[264,128]{1,0:T(8,128)(2,1)S(1)}, u32[]{:S(2)}, u32[]{:S(2)}) collective-permute-start(s16[264,128]{1,0:T(8,128)(2,1)S(1)} %get-tuple-element.34), channel_id=1, source_target_pairs={{0,6},{1,7},{2,0},{3,1},{4,2},{5,3},{6,4},{7,5},{8,14},{9,15},{10,... | collective-permute-start | bytes 202760 | tf_op jit(solution)/shard_map/ppermute | solution.py:35
where the time goes:
time: 121 us; the launch traced here: 119 us
  waiting for transfers between devices  63 us (52%)
  starting transfers between devices  38.7 us (32%)
  Pallas kernels  15 us (12%)
  local copies, waits for them, and re-layouts  1.62 us (1%)
    ppermute x2, waiting for transfers between devices, on_device(): lax.ppermute(q, 'z', [(i, (i + v ^ 1) - v & nz - 1) for i in range(nz)])  39.6 us
    ppermute x7, starting transfers between devices, shifted(): lax.ppermute(array, axis, [(i, (i + by) % size) for i in range(size)])  12.9 us
    ppermute x7, waiting for transfers between devices, shifted(): lax.ppermute(array, axis, [(i, (i + by) % size) for i in range(size)])  11.3 us
    all_to_all x1, starting transfers between devices, on_device(): meta = lax.all_to_all(told, GY, split_axis=0, concat_axis=0, tiled=True)  11.3 us
    all_to_all x1, starting transfers between devices, on_device(): got = lax.all_to_all(sent, GY, split_axis=0, concat_axis=0, tiled=True)  6.72 us
    all_to_all x1, waiting for transfers between devices, on_device(): meta = lax.all_to_all(told, GY, split_axis=0, concat_axis=0, tiled=True)  6.38 us
    ppermute x3, starting transfers between devices, on_device(): lax.ppermute(mine[0], 'gx', [(i, (i + cores * k) % gx) for i in range(gx)])  4.52 us
    ppermute x3, waiting for transfers between devices, on_device(): lax.ppermute(mine[0], 'gx', [(i, (i + cores * k) % gx) for i in range(gx)])  4.48 us
  transfers between devices with their start and end apart: 18, of which 13 were waited for; matrix products, arithmetic and copies ran while one was open for 0% of the time, Pallas kernels for 8%

commit v1 on v0

--- a/solution.py
+++ b/solution.py
@@ -35,11 +35,19 @@
     return lax.ppermute(array, axis, [(i, (i + by) % size) for i in range(size)])
 
 
-def tell_kernel(slots, row_ref, col_ref, work_ref, out_ref, held, sems):
+def tell_kernel(slots, row_ref, col_ref, work_ref, vals_ref, out_ref, tiles_ref, held, sems, tile_sems):
     copies = [
         pltpu.make_async_copy(ref, held.at[i], sems.at[i]) for i, ref in enumerate((row_ref, col_ref, work_ref))
     ]
-    for c in copies:
+    groups = tile_sems.shape[0]
+    size = slots // groups
+    staged = [
+        pltpu.make_async_copy(
+            vals_ref.at[pl.ds(g * size, size)], tiles_ref.at[pl.ds(g * size, size)], tile_sems.at[g]
+        )
+        for g in range(groups)
+    ]
+    for c in (*copies, *staged):
         c.start()
     for c in copies:
         c.wait()
@@ -48,20 +56,7 @@
     for i, pair in enumerate(((row, col), (work, jnp.broadcast_to(count, (1, slots))))):
         line = jnp.concatenate(pair, axis=1)
         out_ref[:, i, :] = jnp.broadcast_to(line, (out_ref.shape[0], 2 * slots))
-
-
-def stage_kernel(vals_ref, out_ref, sems):
-    groups = sems.shape[0]
-    size = vals_ref.shape[0] // groups
-    copies = [
-        pltpu.make_async_copy(
-            vals_ref.at[pl.ds(g * size, size)], out_ref.at[pl.ds(g * size, size)], sems.at[g]
-        )
-        for g in range(groups)
-    ]
-    for c in copies:
-        c.start()
-    for c in copies:
+    for c in staged:
         c.wait()
 
 
@@ -315,15 +310,19 @@
     width = features.shape[1]
     vblocks = features.shape[0] // order
     blocks = peers * vblocks
-    told = pl.pallas_call(
+    told, tiles = pl.pallas_call(
         lambda *refs: tell_kernel(slots, *refs),
-        in_specs=[ANY] * 3,
-        out_specs=VMEM,
-        out_shape=jax.ShapeDtypeStruct((peers, 2, 2 * slots), jnp.int32),
-        scratch_shapes=[pltpu.VMEM((3, slots), jnp.int32), pltpu.SemaphoreType.DMA((3,))],
+        in_specs=[ANY] * 4,
+        out_specs=[VMEM, VMEM],
+        out_shape=[pltpu.HBM((peers, 2, 2 * slots), jnp.int32), vmem(tile_vals.shape, tile_vals.dtype)],
+        scratch_shapes=[
+            pltpu.VMEM((3, slots), jnp.int32),
+            pltpu.SemaphoreType.DMA((3,)),
+            pltpu.SemaphoreType.DMA((8,)),
+        ],
         compiler_params=limit(4),
         name="tell",
-    )(*(in_hbm(t) for t in (tile_row, tile_col, tile_work)))
+    )(*(in_hbm(t) for t in (tile_row, tile_col, tile_work, tile_vals)))
 
     cores = 2
     mine = [features.reshape(vblocks, order, width)]
@@ -333,15 +332,6 @@
     swapped = []
     for f in mine:
         swapped.append(lax.ppermute(f, "gx", [(i, i ^ 1) for i in range(gx)]))
-    tiles = pl.pallas_call(
-        stage_kernel,
-        in_specs=[ANY],
-        out_specs=VMEM,
-        out_shape=vmem(tile_vals.shape, tile_vals.dtype),
-        scratch_shapes=[pltpu.SemaphoreType.DMA((8,))],
-        compiler_params=limit(4),
-        name="stage",
-    )(in_hbm(tile_vals))
     small = jax.ShapeDtypeStruct((owned,), jnp.int32)
     sent = pl.pallas_call(
         lambda *refs: plan_kernel(peers, slots, *refs),

time: 121 us -> 121 us (level)
  blocking collectives: 0 us -> 19.2 us
  starting transfers between devices: 38.7 us -> 26.8 us
  waiting for transfers between devices: 63 us -> 55.1 us
  local copies, waits for them, and re-layouts: 1.62 us -> 4.48 us
  Pallas kernels: 15 us -> 13.3 us
    all_to_all x0 -> x1, blocking collectives: none -> 19.2 us  [on_device(): meta = lax.all_to_all(told, GY, split_axis=0, concat_axis=0, tiled=True)]
    all_to_all x1 -> x0, starting transfers between devices: 11.3 us -> none  [on_device(): meta = lax.all_to_all(told, GY, split_axis=0, concat_axis=0, tiled=True)]
    all_to_all x1 -> x0, waiting for transfers between devices: 6.38 us -> none  [on_device(): meta = lax.all_to_all(told, GY, split_axis=0, concat_axis=0, tiled=True)]
    unnamed x10 -> x14, local copies, waits for them, and re-layouts: 1.62 us -> 4.48 us
    pallas_call x1 -> x0, Pallas kernels: 1.58 us -> none  [on_device(): pl.pallas_call(stage_kernel, in_specs=[ANY], out_specs=VMEM, out_shape=vm...]
    ppermute x2, waiting for transfers between devices: 39.6 us -> 38.1 us  [on_device(): lax.ppermute(q, 'z', [(i, (i + v ^ 1) - v & nz - 1) for i in range(nz)])]
  transfers between devices with their start and end apart: 18 -> 17, of which waited for: 13 -> 12; matrix products, arithmetic and copies ran while one was open for 0% -> 0% of each run, Pallas kernels for 8% -> 7%
where the time goes in v1:
time: 121 us; the launch traced here: 120 us
  waiting for transfers between devices  55.1 us (46%)
  starting transfers between devices  26.8 us (22%)
  blocking collectives  19.2 us (16%)
  Pallas kernels  13.3 us (11%)
  local copies, waits for them, and re-layouts  4.48 us (4%)
    ppermute x2, waiting for transfers between devices, on_device(): lax.ppermute(q, 'z', [(i, (i + v ^ 1) - v & nz - 1) for i in range(nz)])  38.1 us
    all_to_all x1, blocking collectives, on_device(): meta = lax.all_to_all(told, GY, split_axis=0, concat_axis=0, tiled=True)  19.2 us
    ppermute x7, starting transfers between devices, shifted(): lax.ppermute(array, axis, [(i, (i + by) % size) for i in range(size)])  12.9 us
    ppermute x7, waiting for transfers between devices, shifted(): lax.ppermute(array, axis, [(i, (i + by) % size) for i in range(size)])  11.3 us
    all_to_all x1, starting transfers between devices, on_device(): got = lax.all_to_all(sent, GY, split_axis=0, concat_axis=0, tiled=True)  6.05 us
    ppermute x3, starting transfers between devices, on_device(): lax.ppermute(mine[0], 'gx', [(i, (i + cores * k) % gx) for i in range(gx)])  4.52 us
    ppermute x3, waiting for transfers between devices, on_device(): lax.ppermute(mine[0], 'gx', [(i, (i + cores * k) % gx) for i in range(gx)])  4.48 us
    unnamed x14, local copies, waits for them, and re-layouts  4.48 us
  transfers between devices with their start and end apart: 17, of which 12 were waited for; matrix products, arithmetic and copies ran while one was open for 0% of the time, Pallas kernels for 7%

profile of v1, /device:TPU:40, one launch (start us, length us, event | category | flops | bytes accessed | tf_op | source)
XLA Modules:
  0.0 119.8 jit_solution(3849242518245366499)
XLA Ops:
  0.6 2.3 %tell.1 = (s32[32,2,128]{2,1,0:T(2,128)}, bf16[64,128,128]{2,1,0:T(8,128)(2,1)S(1)}) custom-call(s32[64]{0:T(128)} %refs_0_.3, s32[64]{0:T(128)} %refs_1_.3, s32[64]{0:T(128)} %refs_2_.3, bf16[64,128,128]{2,1,0:T(8,128)(2,1)} %refs_3_.1), custom_call_target="tpu_custom_call" | custom-call | tf_op jit(solution)/shard_map/tell/pallas_call | solution.py:313
  2.9 19.2 %all_to_all.10.refs_0_ = s32[32,2,128]{2,1,0:T(2,128)S(1)} all-to-all(s32[32,2,128]{2,1,0:T(2,128)} %get-tuple-element.38), channel_id=1, replica_groups=mesh['gx'=8,'y'=4,'z'=8] {'y','z'}, dimensions={0} | all-to-all | bytes 65536 | tf_op jit(solution)/shard_map/all_to_all | solution.py:331
  22.1 1.5 %plan.1 = bf16[64,128,128]{2,1,0:T(8,128)(2,1)} custom-call(s32[32,2,128]{2,1,0:T(2,128)S(1)} %all_to_all.10.refs_0_, bf16[64,128,128]{2,1,0:T(8,128)(2,1)S(1)} %get-tuple-element.24.refs_3_.refs_1_), custom_call_target="tpu_custom_call" | custom-call | tf_op jit(solution)/shard_map/plan/pallas_call | solution.py:336
  23.6 1.3 %copy-done = bf16[64,128,128]{2,1,0:T(8,128)(2,1)} copy-done((bf16[64,128,128]{2,1,0:T(8,128)(2,1)}, bf16[64,128,128]{2,1,0:T(8,128)(2,1)S(1)}, u32[]{:S(2)}) %copy-start) | copy-done | bytes 2097176
  24.9 6.0 %all-to-all-start.1 = ((bf16[64,128,128]{2,1,0:T(8,128)(2,1)}), bf16[64,128,128]{2,1,0:T(8,128)(2,1)S(1)}, u32[]{:S(2)}, u32[]{:S(2)}) async-start(bf16[64,128,128]{2,1,0:T(8,128)(2,1)} %plan.1), calls=%async_computation.1 | async-start | bytes 4194304 | tf_op jit(solution)/shard_map/all_to_all | solution.py:353
  31.0 2.8 %collective-permute-start.2 = (bf16[2,128,128]{2,1,0:T(8,128)(2,1)S(1)}, bf16[2,128,128]{2,1,0:T(8,128)(2,1)S(1)}, u32[]{:S(2)}, u32[]{:S(2)}) collective-permute-start(bf16[2,128,128]{2,1,0:T(8,128)(2,1)S(1)} %bitcast.1), channel_id=1, source_target_pairs={{0,192},{32,224},{64,0},{96,32},{128,64},{160,96},{192,128},{224,1... | collective-permute-start | bytes 196616 | tf_op jit(solution)/shard_map/ppermute | solution.py:330
  33.8 0.8 collective-permute-start.1
  34.6 0.9 collective-permute-start
  36.0 3.6 %collective-permute-done.1.refs_6_ = bf16[2,128,128]{2,1,0:T(8,128)(2,1)S(1)} collective-permute-done((bf16[2,128,128]{2,1,0:T(8,128)(2,1)S(1)}, bf16[2,128,128]{2,1,0:T(8,128)(2,1)S(1)}, u32[]{:S(2)}, u32[]{:S(2)}) %collective-permute-start.1) | collective-permute-done | bytes 65568 | tf_op jit(solution)/shard_map/ppermute | solution.py:330
  39.6 0.7 collective-permute-done.refs_5_
  40.3 0.6 collective-permute-done.5.refs_10_
  40.9 0.7 collective-permute-done.4.refs_9_
  41.6 1.6 %copy-done.1 = bf16[64,128,128]{2,1,0:T(8,128)(2,1)S(1)} copy-done((bf16[64,128,128]{2,1,0:T(8,128)(2,1)S(1)}, bf16[64,128,128]{2,1,0:T(8,128)(2,1)}, u32[]{:S(2)}) %copy-start.1) | copy-done | bytes 2097176
  43.2 3.6 %products.1 = (f32[32,128,128]{2,1,0:T(8,128)}, s16[2064,128]{1,0:T(8,128)(2,1)}, s16[2064,128]{1,0:T(8,128)(2,1)}) custom-call(s32[64]{0:T(128)S(1)} %copy-done.4, s32[64]{0:T(128)S(1)} %copy-done.5, s32[64]{0:T(128)S(1)} %copy-done.6, bf16[64,128,128]{2,1,0:T(8,128)(2,1)S(1)} %copy-done.1, bf16[2,128,128]{2,1,0:T(8,128)(2,1)S(1)} %bitcast.5, ...), custom_call_target="tpu_custom_call" | custom-call | tf_op jit(solution)/shard_map/products/pallas_call | solution.py:364
  46.8 0.6 collective-permute-start.7
  47.4 2.4 %collective-permute-start.8 = (s16[2064,128]{1,0:T(8,128)(2,1)}, s16[2064,128]{1,0:T(8,128)(2,1)S(1)}, u32[]{:S(2)}, u32[]{:S(2)}) collective-permute-start(s16[2064,128]{1,0:T(8,128)(2,1)} %get-tuple-element.27), channel_id=1, source_target_pairs={{0,7},{1,2},{2,1},{3,4},{4,3},{5,6},{6,5},{7,0},{8,15},{9,10},{10,... | collective-permute-start | bytes 1585160 | tf_op jit(solution)/shard_map/ppermute | solution.py:383
  49.8 37.1 %collective-permute-done.7.refs_1_ = s16[2064,128]{1,0:T(8,128)(2,1)S(1)} collective-permute-done((s16[2064,128]{1,0:T(8,128)(2,1)}, s16[2064,128]{1,0:T(8,128)(2,1)S(1)}, u32[]{:S(2)}, u32[]{:S(2)}) %collective-permute-start.7) | collective-permute-done | bytes 528416 | tf_op jit(solution)/shard_map/ppermute | solution.py:383
  86.9 1.0 collective-permute-done.8.refs_2_
  87.9 1.6 %copy-done.2 = f32[32,128,128]{2,1,0:T(8,128)S(1)} copy-done((f32[32,128,128]{2,1,0:T(8,128)S(1)}, f32[32,128,128]{2,1,0:T(8,128)}, u32[]{:S(2)}) %copy-start.2) | copy-done | bytes 2097176
  90.0 1.6 %collective-permute-start.9 = (s16[1032,128]{1,0:T(8,128)(2,1)S(1)}, s16[1032,128]{1,0:T(8,128)(2,1)S(1)}, u32[]{:S(2)}, u32[]{:S(2)}) collective-permute-start(s16[1032,128]{1,0:T(8,128)(2,1)S(1)} %get-tuple-element.29), channel_id=1, source_target_pairs={{0,8},{8,16},{16,24},{24,0},{1,9},{9,17},{17,25},{25,1},{2,10},{10... | collective-permute-start | bytes 792584 | tf_op jit(solution)/shard_map/ppermute | solution.py:35
  92.1 5.3 %collective-permute-done.9.refs_1_ = s16[1032,128]{1,0:T(8,128)(2,1)S(1)} collective-permute-done((s16[1032,128]{1,0:T(8,128)(2,1)S(1)}, s16[1032,128]{1,0:T(8,128)(2,1)S(1)}, u32[]{:S(2)}, u32[]{:S(2)}) %collective-permute-start.9) | collective-permute-done | bytes 264224 | tf_op jit(solution)/shard_map/ppermute | solution.py:35
  97.4 1.2 %collective-permute-done.10.refs_2_ = s16[1032,128]{1,0:T(8,128)(2,1)S(1)} collective-permute-done((s16[1032,128]{1,0:T(8,128)(2,1)S(1)}, s16[1032,128]{1,0:T(8,128)(2,1)S(1)}, u32[]{:S(2)}, u32[]{:S(2)}) %collective-permute-start.10) | collective-permute-done | bytes 264224 | tf_op jit(solution)/shard_map/ppermute | solution.py:35
  98.8 1.3 %collective-permute-start.11 = (s16[520,128]{1,0:T(8,128)(2,1)S(1)}, s16[520,128]{1,0:T(8,128)(2,1)S(1)}, u32[]{:S(2)}, u32[]{:S(2)}) collective-permute-start(s16[520,128]{1,0:T(8,128)(2,1)S(1)} %get-tuple-element.32), channel_id=1, source_target_pairs={{0,8},{8,16},{16,24},{24,0},{1,9},{9,17},{17,25},{25,1},{2,10},{10... | collective-permute-start | bytes 399368 | tf_op jit(solution)/shard_map/ppermute | solution.py:35
  100.1 0.8 collective-permute-start.12
  100.9 3.0 %collective-permute-done.11.refs_3_ = s16[520,128]{1,0:T(8,128)(2,1)S(1)} collective-permute-done((s16[520,128]{1,0:T(8,128)(2,1)S(1)}, s16[520,128]{1,0:T(8,128)(2,1)S(1)}, u32[]{:S(2)}, u32[]{:S(2)}) %collective-permute-start.11) | collective-permute-done | bytes 133152 | tf_op jit(solution)/shard_map/ppermute | solution.py:35
  103.9 1.2 %collective-permute-done.12.refs_4_ = s16[520,128]{1,0:T(8,128)(2,1)S(1)} collective-permute-done((s16[520,128]{1,0:T(8,128)(2,1)S(1)}, s16[520,128]{1,0:T(8,128)(2,1)S(1)}, u32[]{:S(2)}, u32[]{:S(2)}) %collective-permute-start.12) | collective-permute-done | bytes 133152 | tf_op jit(solution)/shard_map/ppermute | solution.py:35
  105.4 3.5 %collective-permute-start.13 = (s16[264,128]{1,0:T(8,128)(2,1)S(1)}, s16[264,128]{1,0:T(8,128)(2,1)S(1)}, u32[]{:S(2)}, u32[]{:S(2)}) collective-permute-start(s16[264,128]{1,0:T(8,128)(2,1)S(1)} %get-tuple-element.35), channel_id=1, source_target_pairs={{0,2},{1,3},{2,4},{3,5},{4,6},{5,7},{6,0},{7,1},{8,10},{9,11},{10,... | collective-permute-start | bytes 202760 | tf_op jit(solution)/shard_map/ppermute | solution.py:35
  108.8 1.2 %collective-permute-start.14 = (s16[264,128]{1,0:T(8,128)(2,1)S(1)}, s16[264,128]{1,0:T(8,128)(2,1)S(1)}, u32[]{:S(2)}, u32[]{:S(2)}) collective-permute-start(s16[264,128]{1,0:T(8,128)(2,1)S(1)} %get-tuple-element.36), channel_id=1, source_target_pairs={{0,4},{1,5},{2,6},{3,7},{4,0},{5,1},{6,2},{7,3},{8,12},{9,13},{10,... | collective-permute-start | bytes 202760 | tf_op jit(solution)/shard_map/ppermute | solution.py:35
  110.0 4.0 %collective-permute-start.15 = (s16[264,128]{1,0:T(8,128)(2,1)S(1)}, s16[264,128]{1,0:T(8,128)(2,1)S(1)}, u32[]{:S(2)}, u32[]{:S(2)}) collective-permute-start(s16[264,128]{1,0:T(8,128)(2,1)S(1)} %get-tuple-element.37), channel_id=1, source_target_pairs={{0,6},{1,7},{2,0},{3,1},{4,2},{5,3},{6,4},{7,5},{8,14},{9,15},{10,... | collective-permute-start | bytes 202760 | tf_op jit(solution)/shard_map/ppermute | solution.py:35
  114.1 2.8 %list.1 = (s32[32]{0:T(128)}, s32[32]{0:T(128)}, s32[32]{0:T(128)}, s32[32]{0:T(128)S(1)}) custom-call(s32[32,2,128]{2,1,0:T(2,128)S(1)} %all_to_all.10.refs_0_), custom_call_target="tpu_custom_call" | custom-call | tf_op jit(solution)/shard_map/list/pallas_call | solution.py:345
  117.4 0.7 last.1
  118.1 1.5 %keep.1 = bf16[32,128,128]{2,1,0:T(8,128)(2,1)} custom-call(s32[32]{0:T(128)S(1)} %get-tuple-element.39.refs_0_, bf16[64,128,128]{2,1,0:T(8,128)(2,1)S(1)} %all-to-all-done.1.refs_1_), custom_call_target="tpu_custom_call" | custom-call | tf_op jit(solution)/shard_map/keep/pallas_call | solution.py:426
  (26 shorter events, 2.5 us)
Async XLA Ops:
  23.6 1.3 %copy-start = (bf16[64,128,128]{2,1,0:T(8,128)(2,1)}, bf16[64,128,128]{2,1,0:T(8,128)(2,1)S(1)}, u32[]{:S(2)}) copy-start(bf16[64,128,128]{2,1,0:T(8,128)(2,1)S(1)} %get-tuple-element.24.refs_3_.refs_1_) | copy-start | bytes 6291460
  24.9 6.1 %copy-start.3 = (bf16[256,128]{1,0:T(8,128)(2,1)S(1)}, bf16[256,128]{1,0:T(8,128)(2,1)}, u32[]{:S(2)}) copy-start(bf16[256,128]{1,0:T(8,128)(2,1)} %param.5) | copy-start | bytes 196612
  24.9 16.6 %copy-start.4 = (s32[64]{0:T(128)S(1)}, s32[64]{0:T(128)}, u32[]{:S(2)}) copy-start(s32[64]{0:T(128)} %refs_0_.3) | copy-start | bytes 772
  24.9 16.6 %copy-start.5 = (s32[64]{0:T(128)S(1)}, s32[64]{0:T(128)}, u32[]{:S(2)}) copy-start(s32[64]{0:T(128)} %refs_1_.3) | copy-start | bytes 772
  24.9 16.6 %copy-start.6 = (s32[64]{0:T(128)S(1)}, s32[64]{0:T(128)}, u32[]{:S(2)}) copy-start(s32[64]{0:T(128)} %refs_2_.3) | copy-start | bytes 772
  24.9 93.2 %all-to-all-start.1 = ((bf16[64,128,128]{2,1,0:T(8,128)(2,1)}), bf16[64,128,128]{2,1,0:T(8,128)(2,1)S(1)}, u32[]{:S(2)}, u32[]{:S(2)}) async-start(bf16[64,128,128]{2,1,0:T(8,128)(2,1)} %plan.1), calls=%async_computation.1 | async-start | bytes 4194304 | tf_op jit(solution)/shard_map/all_to_all | solution.py:353
  31.0 4.7 %collective-permute-start.2 = (bf16[2,128,128]{2,1,0:T(8,128)(2,1)S(1)}, bf16[2,128,128]{2,1,0:T(8,128)(2,1)S(1)}, u32[]{:S(2)}, u32[]{:S(2)}) collective-permute-start(bf16[2,128,128]{2,1,0:T(8,128)(2,1)S(1)} %bitcast.1), channel_id=1, source_target_pairs={{0,192},{32,224},{64,0},{96,32},{128,64},{160,96},{192,128},{224,1... | collective-permute-start | bytes 196616 | tf_op jit(solution)/shard_map/ppermute | solution.py:330
  33.8 5.8 %collective-permute-start.1 = (bf16[2,128,128]{2,1,0:T(8,128)(2,1)S(1)}, bf16[2,128,128]{2,1,0:T(8,128)(2,1)S(1)}, u32[]{:S(2)}, u32[]{:S(2)}) collective-permute-start(bf16[2,128,128]{2,1,0:T(8,128)(2,1)S(1)} %bitcast.2), channel_id=1, source_target_pairs={{0,128},{32,160},{64,192},{96,224},{128,0},{160,32},{192,64},{224,... | collective-permute-start | bytes 196616 | tf_op jit(solution)/shard_map/ppermute | solution.py:330
  34.6 5.7 %collective-permute-start = (bf16[2,128,128]{2,1,0:T(8,128)(2,1)S(1)}, bf16[2,128,128]{2,1,0:T(8,128)(2,1)S(1)}, u32[]{:S(2)}, u32[]{:S(2)}) collective-permute-start(bf16[2,128,128]{2,1,0:T(8,128)(2,1)S(1)} %bitcast.3), channel_id=1, source_target_pairs={{0,64},{32,96},{64,128},{96,160},{128,192},{160,224},{192,0},{224,... | collective-permute-start | bytes 196616 | tf_op jit(solution)/shard_map/ppermute | solution.py:330
  35.5 4.8 %collective-permute-start.3 = (bf16[2,128,128]{2,1,0:T(8,128)(2,1)S(1)}, bf16[2,128,128]{2,1,0:T(8,128)(2,1)S(1)}, u32[]{:S(2)}, u32[]{:S(2)}) collective-permute-start(bf16[2,128,128]{2,1,0:T(8,128)(2,1)S(1)} %bitcast.4), channel_id=1, source_target_pairs={{0,32},{32,0},{64,96},{96,64},{128,160},{160,128},{192,224},{224,1... | collective-permute-start | bytes 196616 | tf_op jit(solution)/shard_map/ppermute | solution.py:334
  35.7 4.6 %collective-permute-start.6 = (bf16[2,128,128]{2,1,0:T(8,128)(2,1)S(1)}, bf16[2,128,128]{2,1,0:T(8,128)(2,1)S(1)}, u32[]{:S(2)}, u32[]{:S(2)}) collective-permute-start(bf16[2,128,128]{2,1,0:T(8,128)(2,1)S(1)} %collective-permute-done.2.refs_7_), channel_id=1, source_target_pairs={{0,32},{32,0},{64,96},{96,64},{128,160},{160,128},{192,224},{224,1... | collective-permute-start | bytes 196616 | tf_op jit(solution)/shard_map/ppermute | solution.py:334
  39.6 1.3 %collective-permute-start.5 = (bf16[2,128,128]{2,1,0:T(8,128)(2,1)S(1)}, bf16[2,128,128]{2,1,0:T(8,128)(2,1)S(1)}, u32[]{:S(2)}, u32[]{:S(2)}) collective-permute-start(bf16[2,128,128]{2,1,0:T(8,128)(2,1)S(1)} %collective-permute-done.1.refs_6_), channel_id=1, source_target_pairs={{0,32},{32,0},{64,96},{96,64},{128,160},{160,128},{192,224},{224,1... | collective-permute-start | bytes 196616 | tf_op jit(solution)/shard_map/ppermute | solution.py:334
  40.3 1.3 %collective-permute-start.4 = (bf16[2,128,128]{2,1,0:T(8,128)(2,1)S(1)}, bf16[2,128,128]{2,1,0:T(8,128)(2,1)S(1)}, u32[]{:S(2)}, u32[]{:S(2)}) collective-permute-start(bf16[2,128,128]{2,1,0:T(8,128)(2,1)S(1)} %collective-permute-done.refs_5_), channel_id=1, source_target_pairs={{0,32},{32,0},{64,96},{96,64},{128,160},{160,128},{192,224},{224,1... | collective-permute-start | bytes 196616 | tf_op jit(solution)/shard_map/ppermute | solution.py:334
  41.6 1.6 %copy-start.1 = (bf16[64,128,128]{2,1,0:T(8,128)(2,1)S(1)}, bf16[64,128,128]{2,1,0:T(8,128)(2,1)}, u32[]{:S(2)}) copy-start(bf16[64,128,128]{2,1,0:T(8,128)(2,1)} %copy-done) | copy-start | bytes 6291460
  46.8 40.1 %collective-permute-start.7 = (s16[2064,128]{1,0:T(8,128)(2,1)}, s16[2064,128]{1,0:T(8,128)(2,1)S(1)}, u32[]{:S(2)}, u32[]{:S(2)}) collective-permute-start(s16[2064,128]{1,0:T(8,128)(2,1)} %get-tuple-element.26), channel_id=1, source_target_pairs={{0,1},{1,0},{2,3},{3,2},{4,5},{5,4},{6,7},{7,6},{8,9},{9,8},{10,11... | collective-permute-start | bytes 1585160 | tf_op jit(solution)/shard_map/ppermute | solution.py:383
  47.4 40.4 %collective-permute-start.8 = (s16[2064,128]{1,0:T(8,128)(2,1)}, s16[2064,128]{1,0:T(8,128)(2,1)S(1)}, u32[]{:S(2)}, u32[]{:S(2)}) collective-permute-start(s16[2064,128]{1,0:T(8,128)(2,1)} %get-tuple-element.27), channel_id=1, source_target_pairs={{0,7},{1,2},{2,1},{3,4},{4,3},{5,6},{6,5},{7,0},{8,15},{9,10},{10,... | collective-permute-start | bytes 1585160 | tf_op jit(solution)/shard_map/ppermute | solution.py:383
  87.9 1.6 %copy-start.2 = (f32[32,128,128]{2,1,0:T(8,128)S(1)}, f32[32,128,128]{2,1,0:T(8,128)}, u32[]{:S(2)}) copy-start(f32[32,128,128]{2,1,0:T(8,128)} %get-tuple-element.25.refs_0_) | copy-start | bytes 6291460
  90.0 7.4 %collective-permute-start.9 = (s16[1032,128]{1,0:T(8,128)(2,1)S(1)}, s16[1032,128]{1,0:T(8,128)(2,1)S(1)}, u32[]{:S(2)}, u32[]{:S(2)}) collective-permute-start(s16[1032,128]{1,0:T(8,128)(2,1)S(1)} %get-tuple-element.29), channel_id=1, source_target_pairs={{0,8},{8,16},{16,24},{24,0},{1,9},{9,17},{17,25},{25,1},{2,10},{10... | collective-permute-start | bytes 792584 | tf_op jit(solution)/shard_map/ppermute | solution.py:35
  91.5 7.1 %collective-permute-start.10 = (s16[1032,128]{1,0:T(8,128)(2,1)S(1)}, s16[1032,128]{1,0:T(8,128)(2,1)S(1)}, u32[]{:S(2)}, u32[]{:S(2)}) collective-permute-start(s16[1032,128]{1,0:T(8,128)(2,1)S(1)} %get-tuple-element.30), channel_id=1, source_target_pairs={{0,24},{8,0},{16,8},{24,16},{1,25},{9,1},{17,9},{25,17},{2,26},{10... | collective-permute-start | bytes 792584 | tf_op jit(solution)/shard_map/ppermute | solution.py:35
  98.8 5.1 %collective-permute-start.11 = (s16[520,128]{1,0:T(8,128)(2,1)S(1)}, s16[520,128]{1,0:T(8,128)(2,1)S(1)}, u32[]{:S(2)}, u32[]{:S(2)}) collective-permute-start(s16[520,128]{1,0:T(8,128)(2,1)S(1)} %get-tuple-element.32), channel_id=1, source_target_pairs={{0,8},{8,16},{16,24},{24,0},{1,9},{9,17},{17,25},{25,1},{2,10},{10... | collective-permute-start | bytes 399368 | tf_op jit(solution)/shard_map/ppermute | solution.py:35
  100.1 5.0 %collective-permute-start.12 = (s16[520,128]{1,0:T(8,128)(2,1)S(1)}, s16[520,128]{1,0:T(8,128)(2,1)S(1)}, u32[]{:S(2)}, u32[]{:S(2)}) collective-permute-start(s16[520,128]{1,0:T(8,128)(2,1)S(1)} %get-tuple-element.33), channel_id=1, source_target_pairs={{0,24},{8,0},{16,8},{24,16},{1,25},{9,1},{17,9},{25,17},{2,26},{10... | collective-permute-start | bytes 399368 | tf_op jit(solution)/shard_map/ppermute | solution.py:35
  105.4 11.5 %collective-permute-start.13 = (s16[264,128]{1,0:T(8,128)(2,1)S(1)}, s16[264,128]{1,0:T(8,128)(2,1)S(1)}, u32[]{:S(2)}, u32[]{:S(2)}) collective-permute-start(s16[264,128]{1,0:T(8,128)(2,1)S(1)} %get-tuple-element.35), channel_id=1, source_target_pairs={{0,2},{1,3},{2,4},{3,5},{4,6},{5,7},{6,0},{7,1},{8,10},{9,11},{10,... | collective-permute-start | bytes 202760 | tf_op jit(solution)/shard_map/ppermute | solution.py:35
  108.8 8.6 %collective-permute-start.14 = (s16[264,128]{1,0:T(8,128)(2,1)S(1)}, s16[264,128]{1,0:T(8,128)(2,1)S(1)}, u32[]{:S(2)}, u32[]{:S(2)}) collective-permute-start(s16[264,128]{1,0:T(8,128)(2,1)S(1)} %get-tuple-element.36), channel_id=1, source_target_pairs={{0,4},{1,5},{2,6},{3,7},{4,0},{5,1},{6,2},{7,3},{8,12},{9,13},{10,... | collective-permute-start | bytes 202760 | tf_op jit(solution)/shard_map/ppermute | solution.py:35
  110.0 7.4 %collective-permute-start.15 = (s16[264,128]{1,0:T(8,128)(2,1)S(1)}, s16[264,128]{1,0:T(8,128)(2,1)S(1)}, u32[]{:S(2)}, u32[]{:S(2)}) collective-permute-start(s16[264,128]{1,0:T(8,128)(2,1)S(1)} %get-tuple-element.37), channel_id=1, source_target_pairs={{0,6},{1,7},{2,0},{3,1},{4,2},{5,3},{6,4},{7,5},{8,14},{9,15},{10,... | collective-permute-start | bytes 202760 | tf_op jit(solution)/shard_map/ppermute | solution.py:35

commit v2 on v0

--- a/solution.py
+++ b/solution.py
@@ -135,8 +135,7 @@
     exps_ref[pl.ds(row, 1), :] = exponent
 
 
-def product_kernel(gx, gy, groups, steps, row_ref, col_ref, work_ref, tiles, *refs):
-    feats, refs = refs[:gx], refs[gx:]
+def product_kernel(gx, gy, groups, steps, row_ref, col_ref, work_ref, tiles, feats_ref, swap_ref, *refs):
     keep_ref, even_ref, odd_ref, acc, held, made, exps, codes, sems = refs
     slots, order, _ = tiles.shape
     per_step = slots // steps
@@ -147,7 +146,7 @@
     cores = 2
 
     acc[...] = jnp.zeros_like(acc)
-    for k, f in enumerate(feats):
+    for k, f in enumerate((feats_ref, swap_ref)):
         held[pl.ds(k * f.shape[0], f.shape[0])] = f[...]
 
     pattern = lax.broadcasted_iota(jnp.int32, (order, order), 0) * order + lax.broadcasted_iota(
@@ -199,7 +198,7 @@
             return carry
 
         for i in range(parts):
-            lax.fori_loop(i * lines // parts, (i + 1) * lines // parts, code, 0, unroll=2)
+            lax.fori_loop(i * lines // parts, (i + 1) * lines // parts, code, 0, unroll=4)
             if i == parts - 1:
                 store_exps(held_codes, exps, lines, order)
             begin = i * lines * order // parts
@@ -330,9 +329,8 @@
     for k in range(1, gx // cores):
         mine.append(lax.ppermute(mine[0], "gx", [(i, (i + cores * k) % gx) for i in range(gx)]))
     meta = lax.all_to_all(told, GY, split_axis=0, concat_axis=0, tiled=True)
-    swapped = []
-    for f in mine:
-        swapped.append(lax.ppermute(f, "gx", [(i, i ^ 1) for i in range(gx)]))
+    feats = jnp.concatenate(mine)
+    swapped = lax.ppermute(feats, "gx", [(i, i ^ 1) for i in range(gx)])
     tiles = pl.pallas_call(
         stage_kernel,
         in_specs=[ANY],
@@ -362,7 +360,7 @@
     )(meta)
     got = lax.all_to_all(sent, GY, split_axis=0, concat_axis=0, tiled=True)
 
-    steps = 8
+    steps = 4
     span = blocks // ny
     i16 = jnp.int16
 
@@ -373,7 +371,7 @@
     few = span // 2
     keep, even, odd = pl.pallas_call(
         lambda *refs: product_kernel(gx, peers, ny, steps, *refs),
-        in_specs=[SMEM] * 3 + [VMEM] * (1 + gx),
+        in_specs=[SMEM] * 3 + [VMEM] * 3,
         out_specs=[ANY] * 3,
         out_shape=[pltpu.HBM((blocks // 2, order, width), jnp.float32)]
         + [pltpu.HBM((lines * order + lines, width), i16)] * 2,
@@ -387,7 +385,7 @@
         ],
         compiler_params=limit(16),
         name="products",
-    )(tile_row, tile_col, tile_work, *(in_vmem(f) for f in (tiles, *mine, *swapped)))
+    )(tile_row, tile_col, tile_work, *(in_vmem(f) for f in (tiles, feats, swapped)))
     near = []
     for v, q in enumerate((even, odd)):
         near.append(lax.ppermute(q, "z", [(i, ((i + v) ^ 1) - v & nz - 1) for i in range(nz)]))

time: 121 us -> 121 us (level)
  transfers between devices with their start and end apart: 18 -> 15, of which waited for: 13 -> 12; matrix products, arithmetic and copies ran while one was open for 0% -> 0% of each run, Pallas kernels for 8% -> 8%
where the time goes in v2:
time: 121 us; the launch traced here: 119 us
  waiting for transfers between devices  63.2 us (52%)
  starting transfers between devices  38.6 us (32%)
  Pallas kernels  15 us (12%)
  local copies, waits for them, and re-layouts  1.62 us (1%)
    ppermute x2, waiting for transfers between devices, on_device(): lax.ppermute(q, 'z', [(i, (i + v ^ 1) - v & nz - 1) for i in range(nz)])  39.2 us
    ppermute x7, starting transfers between devices, shifted(): lax.ppermute(array, axis, [(i, (i + by) % size) for i in range(size)])  12.9 us
    ppermute x7, waiting for transfers between devices, shifted(): lax.ppermute(array, axis, [(i, (i + by) % size) for i in range(size)])  11.3 us
    all_to_all x1, starting transfers between devices, on_device(): meta = lax.all_to_all(told, GY, split_axis=0, concat_axis=0, tiled=True)  11.3 us
    all_to_all x1, starting transfers between devices, on_device(): got = lax.all_to_all(sent, GY, split_axis=0, concat_axis=0, tiled=True)  6.73 us
    all_to_all x1, waiting for transfers between devices, on_device(): meta = lax.all_to_all(told, GY, split_axis=0, concat_axis=0, tiled=True)  6.38 us
    ppermute x3, waiting for transfers between devices, on_device(): lax.ppermute(mine[0], 'gx', [(i, (i + cores * k) % gx) for i in range(gx)])  4.78 us
    ppermute x3, starting transfers between devices, on_device(): lax.ppermute(mine[0], 'gx', [(i, (i + cores * k) % gx) for i in range(gx)])  4.52 us
  transfers between devices with their start and end apart: 15, of which 12 were waited for; matrix products, arithmetic and copies ran while one was open for 0% of the time, Pallas kernels for 8%

profile of v2, /device:TPU:40, one launch (start us, length us, event | category | flops | bytes accessed | tf_op | source)
XLA Modules:
  0.0 119.2 jit_solution(9306180063566903042)
XLA Ops:
  0.6 1.4 %tell.1 = s32[32,2,128]{2,1,0:T(2,128)} custom-call(s32[64]{0:T(128)} %refs_0_.3, s32[64]{0:T(128)} %refs_1_.3, s32[64]{0:T(128)} %refs_2_.3), custom_call_target="tpu_custom_call" | custom-call | tf_op jit(solution)/shard_map/tell/pallas_call | solution.py:317
  2.1 11.3 %all-to-all-start = ((s32[32,2,128]{2,1,0:T(2,128)}), s32[32,2,128]{2,1,0:T(2,128)S(1)}, u32[]{:S(2)}, u32[]{:S(2)}) async-start(s32[32,2,128]{2,1,0:T(2,128)} %tell.1), calls=%async_computation | async-start | bytes 65536 | tf_op jit(solution)/shard_map/all_to_all | solution.py:331
  13.3 1.6 %stage.1.refs_3_.refs_1_ = bf16[64,128,128]{2,1,0:T(8,128)(2,1)S(1)} custom-call(bf16[64,128,128]{2,1,0:T(8,128)(2,1)} %vals_ref.1), custom_call_target="tpu_custom_call" | custom-call | tf_op jit(solution)/shard_map/stage/pallas_call | solution.py:334
  14.9 6.4 %all-to-all-done.refs_0_ = s32[32,2,128]{2,1,0:T(2,128)S(1)} async-done(((s32[32,2,128]{2,1,0:T(2,128)}), s32[32,2,128]{2,1,0:T(2,128)S(1)}, u32[]{:S(2)}, u32[]{:S(2)}) %all-to-all-start) | async-done | bytes 32800 | tf_op jit(solution)/shard_map/all_to_all | solution.py:331
  21.3 1.4 %plan.1 = bf16[64,128,128]{2,1,0:T(8,128)(2,1)} custom-call(s32[32,2,128]{2,1,0:T(2,128)S(1)} %all-to-all-done.refs_0_, bf16[64,128,128]{2,1,0:T(8,128)(2,1)S(1)} %stage.1.refs_3_.refs_1_), custom_call_target="tpu_custom_call" | custom-call | tf_op jit(solution)/shard_map/plan/pallas_call | solution.py:344
  22.8 6.7 %all-to-all-start.1 = ((bf16[64,128,128]{2,1,0:T(8,128)(2,1)}), bf16[64,128,128]{2,1,0:T(8,128)(2,1)}, u32[]{:S(2)}, u32[]{:S(2)}) async-start(bf16[64,128,128]{2,1,0:T(8,128)(2,1)} %plan.1), calls=%async_computation.1 | async-start | bytes 4194304 | tf_op jit(solution)/shard_map/all_to_all | solution.py:361
  29.6 2.8 %collective-permute-start.2 = (bf16[2,128,128]{2,1,0:T(8,128)(2,1)S(1)}, bf16[2,128,128]{2,1,0:T(8,128)(2,1)S(1)}, u32[]{:S(2)}, u32[]{:S(2)}) collective-permute-start(bf16[2,128,128]{2,1,0:T(8,128)(2,1)S(1)} %bitcast.1), channel_id=1, source_target_pairs={{0,192},{32,224},{64,0},{96,32},{128,64},{160,96},{192,128},{224,1... | collective-permute-start | bytes 196616 | tf_op jit(solution)/shard_map/ppermute | solution.py:330
  32.4 0.8 collective-permute-start.1
  33.2 0.9 collective-permute-start
  34.3 3.9 %collective-permute-done.1 = bf16[2,128,128]{2,1,0:T(8,128)(2,1)S(1)} collective-permute-done((bf16[2,128,128]{2,1,0:T(8,128)(2,1)S(1)}, bf16[2,128,128]{2,1,0:T(8,128)(2,1)S(1)}, u32[]{:S(2)}, u32[]{:S(2)}) %collective-permute-start.1) | collective-permute-done | bytes 65568 | tf_op jit(solution)/shard_map/ppermute | solution.py:330
  38.2 0.7 collective-permute-done
  39.0 1.5 %collective-permute-done.3.refs_5_ = bf16[8,128,128]{2,1,0:T(8,128)(2,1)S(1)} collective-permute-done((bf16[8,128,128]{2,1,0:T(8,128)(2,1)S(1)}, bf16[8,128,128]{2,1,0:T(8,128)(2,1)S(1)}, u32[]{:S(2)}, u32[]{:S(2)}) %collective-permute-start.3) | collective-permute-done | bytes 262176 | tf_op jit(solution)/shard_map/ppermute | solution.py:333
  40.5 3.6 %products.1 = (f32[32,128,128]{2,1,0:T(8,128)}, s16[2064,128]{1,0:T(8,128)(2,1)}, s16[2064,128]{1,0:T(8,128)(2,1)}) custom-call(s32[64]{0:T(128)S(1)} %copy-done.1, s32[64]{0:T(128)S(1)} %copy-done.2, s32[64]{0:T(128)S(1)} %copy-done.3, bf16[64,128,128]{2,1,0:T(8,128)(2,1)S(1)} %stage.1.refs_3_.refs_1_, bf16[8,128,128]{2,1,0:T(8,128)(2,1)S(1)} %pad_maximum_fusion.refs_4_, ...), custom_call_target="tpu_custom_call" | custom-call | tf_op jit(solution)/shard_map/products/pallas_call | solution.py:372
  44.1 0.6 collective-permute-start.4
  44.8 2.4 %collective-permute-start.5 = (s16[2064,128]{1,0:T(8,128)(2,1)}, s16[2064,128]{1,0:T(8,128)(2,1)S(1)}, u32[]{:S(2)}, u32[]{:S(2)}) collective-permute-start(s16[2064,128]{1,0:T(8,128)(2,1)} %get-tuple-element.24), channel_id=1, source_target_pairs={{0,7},{1,2},{2,1},{3,4},{4,3},{5,6},{6,5},{7,0},{8,15},{9,10},{10,... | collective-permute-start | bytes 1585160 | tf_op jit(solution)/shard_map/ppermute | solution.py:391
  47.1 38.3 %collective-permute-done.4.refs_1_ = s16[2064,128]{1,0:T(8,128)(2,1)S(1)} collective-permute-done((s16[2064,128]{1,0:T(8,128)(2,1)}, s16[2064,128]{1,0:T(8,128)(2,1)S(1)}, u32[]{:S(2)}, u32[]{:S(2)}) %collective-permute-start.4) | collective-permute-done | bytes 528416 | tf_op jit(solution)/shard_map/ppermute | solution.py:391
  85.4 1.0 collective-permute-done.5.refs_2_
  86.4 1.6 %copy-done = f32[32,128,128]{2,1,0:T(8,128)S(1)} copy-done((f32[32,128,128]{2,1,0:T(8,128)S(1)}, f32[32,128,128]{2,1,0:T(8,128)}, u32[]{:S(2)}) %copy-start) | copy-done | bytes 2097176
  88.5 1.6 %collective-permute-start.6 = (s16[1032,128]{1,0:T(8,128)(2,1)S(1)}, s16[1032,128]{1,0:T(8,128)(2,1)S(1)}, u32[]{:S(2)}, u32[]{:S(2)}) collective-permute-start(s16[1032,128]{1,0:T(8,128)(2,1)S(1)} %get-tuple-element.26), channel_id=1, source_target_pairs={{0,8},{8,16},{16,24},{24,0},{1,9},{9,17},{17,25},{25,1},{2,10},{10... | collective-permute-start | bytes 792584 | tf_op jit(solution)/shard_map/ppermute | solution.py:35
  90.6 5.3 %collective-permute-done.6.refs_1_ = s16[1032,128]{1,0:T(8,128)(2,1)S(1)} collective-permute-done((s16[1032,128]{1,0:T(8,128)(2,1)S(1)}, s16[1032,128]{1,0:T(8,128)(2,1)S(1)}, u32[]{:S(2)}, u32[]{:S(2)}) %collective-permute-start.6) | collective-permute-done | bytes 264224 | tf_op jit(solution)/shard_map/ppermute | solution.py:35
  95.9 1.2 %collective-permute-done.7.refs_2_ = s16[1032,128]{1,0:T(8,128)(2,1)S(1)} collective-permute-done((s16[1032,128]{1,0:T(8,128)(2,1)S(1)}, s16[1032,128]{1,0:T(8,128)(2,1)S(1)}, u32[]{:S(2)}, u32[]{:S(2)}) %collective-permute-start.7) | collective-permute-done | bytes 264224 | tf_op jit(solution)/shard_map/ppermute | solution.py:35
  97.3 1.3 %collective-permute-start.8 = (s16[520,128]{1,0:T(8,128)(2,1)S(1)}, s16[520,128]{1,0:T(8,128)(2,1)S(1)}, u32[]{:S(2)}, u32[]{:S(2)}) collective-permute-start(s16[520,128]{1,0:T(8,128)(2,1)S(1)} %get-tuple-element.29), channel_id=1, source_target_pairs={{0,8},{8,16},{16,24},{24,0},{1,9},{9,17},{17,25},{25,1},{2,10},{10... | collective-permute-start | bytes 399368 | tf_op jit(solution)/shard_map/ppermute | solution.py:35
  98.6 0.8 collective-permute-start.9
  99.4 3.0 %collective-permute-done.8.refs_3_ = s16[520,128]{1,0:T(8,128)(2,1)S(1)} collective-permute-done((s16[520,128]{1,0:T(8,128)(2,1)S(1)}, s16[520,128]{1,0:T(8,128)(2,1)S(1)}, u32[]{:S(2)}, u32[]{:S(2)}) %collective-permute-start.8) | collective-permute-done | bytes 133152 | tf_op jit(solution)/shard_map/ppermute | solution.py:35
  102.4 1.2 %collective-permute-done.9.refs_4_ = s16[520,128]{1,0:T(8,128)(2,1)S(1)} collective-permute-done((s16[520,128]{1,0:T(8,128)(2,1)S(1)}, s16[520,128]{1,0:T(8,128)(2,1)S(1)}, u32[]{:S(2)}, u32[]{:S(2)}) %collective-permute-start.9) | collective-permute-done | bytes 133152 | tf_op jit(solution)/shard_map/ppermute | solution.py:35
  103.9 3.5 %collective-permute-start.10 = (s16[264,128]{1,0:T(8,128)(2,1)S(1)}, s16[264,128]{1,0:T(8,128)(2,1)S(1)}, u32[]{:S(2)}, u32[]{:S(2)}) collective-permute-start(s16[264,128]{1,0:T(8,128)(2,1)S(1)} %get-tuple-element.32), channel_id=1, source_target_pairs={{0,2},{1,3},{2,4},{3,5},{4,6},{5,7},{6,0},{7,1},{8,10},{9,11},{10,... | collective-permute-start | bytes 202760 | tf_op jit(solution)/shard_map/ppermute | solution.py:35
  107.3 1.2 %collective-permute-start.11 = (s16[264,128]{1,0:T(8,128)(2,1)S(1)}, s16[264,128]{1,0:T(8,128)(2,1)S(1)}, u32[]{:S(2)}, u32[]{:S(2)}) collective-permute-start(s16[264,128]{1,0:T(8,128)(2,1)S(1)} %get-tuple-element.33), channel_id=1, source_target_pairs={{0,4},{1,5},{2,6},{3,7},{4,0},{5,1},{6,2},{7,3},{8,12},{9,13},{10,... | collective-permute-start | bytes 202760 | tf_op jit(solution)/shard_map/ppermute | solution.py:35
  108.5 4.0 %collective-permute-start.12 = (s16[264,128]{1,0:T(8,128)(2,1)S(1)}, s16[264,128]{1,0:T(8,128)(2,1)S(1)}, u32[]{:S(2)}, u32[]{:S(2)}) collective-permute-start(s16[264,128]{1,0:T(8,128)(2,1)S(1)} %get-tuple-element.34), channel_id=1, source_target_pairs={{0,6},{1,7},{2,0},{3,1},{4,2},{5,3},{6,4},{7,5},{8,14},{9,15},{10,... | collective-permute-start | bytes 202760 | tf_op jit(solution)/shard_map/ppermute | solution.py:35
  112.6 2.8 %list.1 = (s32[32]{0:T(128)}, s32[32]{0:T(128)}, s32[32]{0:T(128)}, s32[32]{0:T(128)S(1)}) custom-call(s32[32,2,128]{2,1,0:T(2,128)S(1)} %all-to-all-done.refs_0_), custom_call_target="tpu_custom_call" | custom-call | tf_op jit(solution)/shard_map/list/pallas_call | solution.py:353
  115.4 0.5 collective-permute-done.11.refs_2_
  115.9 0.7 last.1
  116.6 2.6 %keep.1 = bf16[32,128,128]{2,1,0:T(8,128)(2,1)} custom-call(s32[32]{0:T(128)S(1)} %get-tuple-element.35.refs_0_, bf16[64,128,128]{2,1,0:T(8,128)(2,1)} %all-to-all-done.1.refs_1_), custom_call_target="tpu_custom_call" | custom-call | tf_op jit(solution)/shard_map/keep/pallas_call | solution.py:434
  (19 shorter events, 1.8 us)
Async XLA Ops:
  2.1 19.2 %all-to-all-start = ((s32[32,2,128]{2,1,0:T(2,128)}), s32[32,2,128]{2,1,0:T(2,128)S(1)}, u32[]{:S(2)}, u32[]{:S(2)}) async-start(s32[32,2,128]{2,1,0:T(2,128)} %tell.1), calls=%async_computation | async-start | bytes 65536 | tf_op jit(solution)/shard_map/all_to_all | solution.py:331
  22.8 6.8 %copy-start.4 = (bf16[256,128]{1,0:T(8,128)(2,1)S(1)}, bf16[256,128]{1,0:T(8,128)(2,1)}, u32[]{:S(2)}) copy-start(bf16[256,128]{1,0:T(8,128)(2,1)} %param.5) | copy-start | bytes 196612
  22.8 17.8 %copy-start.1 = (s32[64]{0:T(128)S(1)}, s32[64]{0:T(128)}, u32[]{:S(2)}) copy-start(s32[64]{0:T(128)} %refs_0_.3) | copy-start | bytes 772
  22.8 17.8 %copy-start.2 = (s32[64]{0:T(128)S(1)}, s32[64]{0:T(128)}, u32[]{:S(2)}) copy-start(s32[64]{0:T(128)} %refs_1_.3) | copy-start | bytes 772
  22.8 17.7 %copy-start.3 = (s32[64]{0:T(128)S(1)}, s32[64]{0:T(128)}, u32[]{:S(2)}) copy-start(s32[64]{0:T(128)} %refs_2_.3) | copy-start | bytes 772
  22.8 93.8 %all-to-all-start.1 = ((bf16[64,128,128]{2,1,0:T(8,128)(2,1)}), bf16[64,128,128]{2,1,0:T(8,128)(2,1)}, u32[]{:S(2)}, u32[]{:S(2)}) async-start(bf16[64,128,128]{2,1,0:T(8,128)(2,1)} %plan.1), calls=%async_computation.1 | async-start | bytes 4194304 | tf_op jit(solution)/shard_map/all_to_all | solution.py:361
  29.6 4.7 %collective-permute-start.2 = (bf16[2,128,128]{2,1,0:T(8,128)(2,1)S(1)}, bf16[2,128,128]{2,1,0:T(8,128)(2,1)S(1)}, u32[]{:S(2)}, u32[]{:S(2)}) collective-permute-start(bf16[2,128,128]{2,1,0:T(8,128)(2,1)S(1)} %bitcast.1), channel_id=1, source_target_pairs={{0,192},{32,224},{64,0},{96,32},{128,64},{160,96},{192,128},{224,1... | collective-permute-start | bytes 196616 | tf_op jit(solution)/shard_map/ppermute | solution.py:330
  32.4 5.8 %collective-permute-start.1 = (bf16[2,128,128]{2,1,0:T(8,128)(2,1)S(1)}, bf16[2,128,128]{2,1,0:T(8,128)(2,1)S(1)}, u32[]{:S(2)}, u32[]{:S(2)}) collective-permute-start(bf16[2,128,128]{2,1,0:T(8,128)(2,1)S(1)} %bitcast.2), channel_id=1, source_target_pairs={{0,128},{32,160},{64,192},{96,224},{128,0},{160,32},{192,64},{224,... | collective-permute-start | bytes 196616 | tf_op jit(solution)/shard_map/ppermute | solution.py:330
  33.2 5.7 %collective-permute-start = (bf16[2,128,128]{2,1,0:T(8,128)(2,1)S(1)}, bf16[2,128,128]{2,1,0:T(8,128)(2,1)S(1)}, u32[]{:S(2)}, u32[]{:S(2)}) collective-permute-start(bf16[2,128,128]{2,1,0:T(8,128)(2,1)S(1)} %bitcast.3), channel_id=1, source_target_pairs={{0,64},{32,96},{64,128},{96,160},{128,192},{160,224},{192,0},{224,... | collective-permute-start | bytes 196616 | tf_op jit(solution)/shard_map/ppermute | solution.py:330
  38.9 1.6 %collective-permute-start.3 = (bf16[8,128,128]{2,1,0:T(8,128)(2,1)S(1)}, bf16[8,128,128]{2,1,0:T(8,128)(2,1)S(1)}, u32[]{:S(2)}, u32[]{:S(2)}) collective-permute-start(bf16[8,128,128]{2,1,0:T(8,128)(2,1)S(1)} %pad_maximum_fusion.refs_4_), channel_id=1, source_target_pairs={{0,32},{32,0},{64,96},{96,64},{128,160},{160,128},{192,224},{224,1... | collective-permute-start | bytes 786440 | tf_op jit(solution)/shard_map/ppermute | solution.py:333
  44.1 41.3 %collective-permute-start.4 = (s16[2064,128]{1,0:T(8,128)(2,1)}, s16[2064,128]{1,0:T(8,128)(2,1)S(1)}, u32[]{:S(2)}, u32[]{:S(2)}) collective-permute-start(s16[2064,128]{1,0:T(8,128)(2,1)} %get-tuple-element.23), channel_id=1, source_target_pairs={{0,1},{1,0},{2,3},{3,2},{4,5},{5,4},{6,7},{7,6},{8,9},{9,8},{10,11... | collective-permute-start | bytes 1585160 | tf_op jit(solution)/shard_map/ppermute | solution.py:391
  44.8 41.6 %collective-permute-start.5 = (s16[2064,128]{1,0:T(8,128)(2,1)}, s16[2064,128]{1,0:T(8,128)(2,1)S(1)}, u32[]{:S(2)}, u32[]{:S(2)}) collective-permute-start(s16[2064,128]{1,0:T(8,128)(2,1)} %get-tuple-element.24), channel_id=1, source_target_pairs={{0,7},{1,2},{2,1},{3,4},{4,3},{5,6},{6,5},{7,0},{8,15},{9,10},{10,... | collective-permute-start | bytes 1585160 | tf_op jit(solution)/shard_map/ppermute | solution.py:391
  86.4 1.6 %copy-start = (f32[32,128,128]{2,1,0:T(8,128)S(1)}, f32[32,128,128]{2,1,0:T(8,128)}, u32[]{:S(2)}) copy-start(f32[32,128,128]{2,1,0:T(8,128)} %get-tuple-element.22.refs_0_) | copy-start | bytes 6291460
  88.5 7.4 %collective-permute-start.6 = (s16[1032,128]{1,0:T(8,128)(2,1)S(1)}, s16[1032,128]{1,0:T(8,128)(2,1)S(1)}, u32[]{:S(2)}, u32[]{:S(2)}) collective-permute-start(s16[1032,128]{1,0:T(8,128)(2,1)S(1)} %get-tuple-element.26), channel_id=1, source_target_pairs={{0,8},{8,16},{16,24},{24,0},{1,9},{9,17},{17,25},{25,1},{2,10},{10... | collective-permute-start | bytes 792584 | tf_op jit(solution)/shard_map/ppermute | solution.py:35
  90.0 7.1 %collective-permute-start.7 = (s16[1032,128]{1,0:T(8,128)(2,1)S(1)}, s16[1032,128]{1,0:T(8,128)(2,1)S(1)}, u32[]{:S(2)}, u32[]{:S(2)}) collective-permute-start(s16[1032,128]{1,0:T(8,128)(2,1)S(1)} %get-tuple-element.27), channel_id=1, source_target_pairs={{0,24},{8,0},{16,8},{24,16},{1,25},{9,1},{17,9},{25,17},{2,26},{10... | collective-permute-start | bytes 792584 | tf_op jit(solution)/shard_map/ppermute | solution.py:35
  97.3 5.1 %collective-permute-start.8 = (s16[520,128]{1,0:T(8,128)(2,1)S(1)}, s16[520,128]{1,0:T(8,128)(2,1)S(1)}, u32[]{:S(2)}, u32[]{:S(2)}) collective-permute-start(s16[520,128]{1,0:T(8,128)(2,1)S(1)} %get-tuple-element.29), channel_id=1, source_target_pairs={{0,8},{8,16},{16,24},{24,0},{1,9},{9,17},{17,25},{25,1},{2,10},{10... | collective-permute-start | bytes 399368 | tf_op jit(solution)/shard_map/ppermute | solution.py:35
  98.6 5.0 %collective-permute-start.9 = (s16[520,128]{1,0:T(8,128)(2,1)S(1)}, s16[520,128]{1,0:T(8,128)(2,1)S(1)}, u32[]{:S(2)}, u32[]{:S(2)}) collective-permute-start(s16[520,128]{1,0:T(8,128)(2,1)S(1)} %get-tuple-element.30), channel_id=1, source_target_pairs={{0,24},{8,0},{16,8},{24,16},{1,25},{9,1},{17,9},{25,17},{2,26},{10... | collective-permute-start | bytes 399368 | tf_op jit(solution)/shard_map/ppermute | solution.py:35
  103.9 11.5 %collective-permute-start.10 = (s16[264,128]{1,0:T(8,128)(2,1)S(1)}, s16[264,128]{1,0:T(8,128)(2,1)S(1)}, u32[]{:S(2)}, u32[]{:S(2)}) collective-permute-start(s16[264,128]{1,0:T(8,128)(2,1)S(1)} %get-tuple-element.32), channel_id=1, source_target_pairs={{0,2},{1,3},{2,4},{3,5},{4,6},{5,7},{6,0},{7,1},{8,10},{9,11},{10,... | collective-permute-start | bytes 202760 | tf_op jit(solution)/shard_map/ppermute | solution.py:35
  107.3 8.6 %collective-permute-start.11 = (s16[264,128]{1,0:T(8,128)(2,1)S(1)}, s16[264,128]{1,0:T(8,128)(2,1)S(1)}, u32[]{:S(2)}, u32[]{:S(2)}) collective-permute-start(s16[264,128]{1,0:T(8,128)(2,1)S(1)} %get-tuple-element.33), channel_id=1, source_target_pairs={{0,4},{1,5},{2,6},{3,7},{4,0},{5,1},{6,2},{7,3},{8,12},{9,13},{10,... | collective-permute-start | bytes 202760 | tf_op jit(solution)/shard_map/ppermute | solution.py:35
  108.5 7.4 %collective-permute-start.12 = (s16[264,128]{1,0:T(8,128)(2,1)S(1)}, s16[264,128]{1,0:T(8,128)(2,1)S(1)}, u32[]{:S(2)}, u32[]{:S(2)}) collective-permute-start(s16[264,128]{1,0:T(8,128)(2,1)S(1)} %get-tuple-element.34), channel_id=1, source_target_pairs={{0,6},{1,7},{2,0},{3,1},{4,2},{5,3},{6,4},{7,5},{8,14},{9,15},{10,... | collective-permute-start | bytes 202760 | tf_op jit(solution)/shard_map/ppermute | solution.py:35

commit v3 on v2

--- a/solution.py
+++ b/solution.py
@@ -88,7 +88,7 @@
             ).start()
         return carry
 
-    lax.fori_loop(0, peers, start, 0, unroll=8)
+    lax.fori_loop(0, peers, start, 0, unroll=True)
     pltpu.make_async_copy(vals_ref, sent_ref, sems.at[0]).wait()
 
 
@@ -120,7 +120,7 @@
         pltpu.make_async_copy(got_ref.at[slot_ref[k]], out_ref.at[k], sems.at[0]).start()
         return carry
 
-    lax.fori_loop(0, owned, start, 0)
+    lax.fori_loop(0, owned, start, 0, unroll=True)
     pltpu.make_async_copy(got_ref.at[pl.ds(0, owned)], out_ref, sems.at[0]).wait()
 
 
@@ -198,7 +198,7 @@
             return carry
 
         for i in range(parts):
-            lax.fori_loop(i * lines // parts, (i + 1) * lines // parts, code, 0, unroll=4)
+            lax.fori_loop(i * lines // parts, (i + 1) * lines // parts, code, 0, unroll=2)
             if i == parts - 1:
                 store_exps(held_codes, exps, lines, order)
             begin = i * lines * order // parts
@@ -360,7 +360,7 @@
     )(meta)
     got = lax.all_to_all(sent, GY, split_axis=0, concat_axis=0, tiled=True)
 
-    steps = 4
+    steps = 8
     span = blocks // ny
     i16 = jnp.int16
 

time: 121 us -> 121 us (level)
  no operation moved by 1% of the time
where the time goes in v3:
time: 121 us; the launch traced here: 119 us
  waiting for transfers between devices  63.2 us (52%)
  starting transfers between devices  38.6 us (32%)
  Pallas kernels  15 us (12%)
  local copies, waits for them, and re-layouts  1.62 us (1%)
    ppermute x2, waiting for transfers between devices, on_device(): lax.ppermute(q, 'z', [(i, (i + v ^ 1) - v & nz - 1) for i in range(nz)])  39.2 us
    ppermute x7, starting transfers between devices, shifted(): lax.ppermute(array, axis, [(i, (i + by) % size) for i in range(size)])  12.9 us
    ppermute x7, waiting for transfers between devices, shifted(): lax.ppermute(array, axis, [(i, (i + by) % size) for i in range(size)])  11.3 us
    all_to_all x1, starting transfers between devices, on_device(): meta = lax.all_to_all(told, GY, split_axis=0, concat_axis=0, tiled=True)  11.3 us
    all_to_all x1, starting transfers between devices, on_device(): got = lax.all_to_all(sent, GY, split_axis=0, concat_axis=0, tiled=True)  6.73 us
    all_to_all x1, waiting for transfers between devices, on_device(): meta = lax.all_to_all(told, GY, split_axis=0, concat_axis=0, tiled=True)  6.38 us
    ppermute x3, waiting for transfers between devices, on_device(): lax.ppermute(mine[0], 'gx', [(i, (i + cores * k) % gx) for i in range(gx)])  4.78 us
    ppermute x3, starting transfers between devices, on_device(): lax.ppermute(mine[0], 'gx', [(i, (i + cores * k) % gx) for i in range(gx)])  4.52 us
  transfers between devices with their start and end apart: 15, of which 12 were waited for; matrix products, arithmetic and copies ran while one was open for 0% of the time, Pallas kernels for 8%

profile of v3, /device:TPU:40, one launch (start us, length us, event | category | flops | bytes accessed | tf_op | source)
XLA Modules:
  0.0 119.2 jit_solution(10506441962533054942)
XLA Ops:
  0.6 1.4 %tell.1 = s32[32,2,128]{2,1,0:T(2,128)} custom-call(s32[64]{0:T(128)} %refs_0_.3, s32[64]{0:T(128)} %refs_1_.3, s32[64]{0:T(128)} %refs_2_.3), custom_call_target="tpu_custom_call" | custom-call | tf_op jit(solution)/shard_map/tell/pallas_call | solution.py:317
  2.1 11.3 %all-to-all-start = ((s32[32,2,128]{2,1,0:T(2,128)}), s32[32,2,128]{2,1,0:T(2,128)S(1)}, u32[]{:S(2)}, u32[]{:S(2)}) async-start(s32[32,2,128]{2,1,0:T(2,128)} %tell.1), calls=%async_computation | async-start | bytes 65536 | tf_op jit(solution)/shard_map/all_to_all | solution.py:331
  13.3 1.6 %stage.1.refs_3_.refs_1_ = bf16[64,128,128]{2,1,0:T(8,128)(2,1)S(1)} custom-call(bf16[64,128,128]{2,1,0:T(8,128)(2,1)} %vals_ref.1), custom_call_target="tpu_custom_call" | custom-call | tf_op jit(solution)/shard_map/stage/pallas_call | solution.py:334
  14.9 6.4 %all-to-all-done.refs_0_ = s32[32,2,128]{2,1,0:T(2,128)S(1)} async-done(((s32[32,2,128]{2,1,0:T(2,128)}), s32[32,2,128]{2,1,0:T(2,128)S(1)}, u32[]{:S(2)}, u32[]{:S(2)}) %all-to-all-start) | async-done | bytes 32800 | tf_op jit(solution)/shard_map/all_to_all | solution.py:331
  21.3 1.4 %plan.1 = bf16[64,128,128]{2,1,0:T(8,128)(2,1)} custom-call(s32[32,2,128]{2,1,0:T(2,128)S(1)} %all-to-all-done.refs_0_, bf16[64,128,128]{2,1,0:T(8,128)(2,1)S(1)} %stage.1.refs_3_.refs_1_), custom_call_target="tpu_custom_call" | custom-call | tf_op jit(solution)/shard_map/plan/pallas_call | solution.py:344
  22.8 6.7 %all-to-all-start.1 = ((bf16[64,128,128]{2,1,0:T(8,128)(2,1)}), bf16[64,128,128]{2,1,0:T(8,128)(2,1)}, u32[]{:S(2)}, u32[]{:S(2)}) async-start(bf16[64,128,128]{2,1,0:T(8,128)(2,1)} %plan.1), calls=%async_computation.1 | async-start | bytes 4194304 | tf_op jit(solution)/shard_map/all_to_all | solution.py:361
  29.6 2.8 %collective-permute-start.2 = (bf16[2,128,128]{2,1,0:T(8,128)(2,1)S(1)}, bf16[2,128,128]{2,1,0:T(8,128)(2,1)S(1)}, u32[]{:S(2)}, u32[]{:S(2)}) collective-permute-start(bf16[2,128,128]{2,1,0:T(8,128)(2,1)S(1)} %bitcast.1), channel_id=1, source_target_pairs={{0,192},{32,224},{64,0},{96,32},{128,64},{160,96},{192,128},{224,1... | collective-permute-start | bytes 196616 | tf_op jit(solution)/shard_map/ppermute | solution.py:330
  32.4 0.8 collective-permute-start.1
  33.2 0.9 collective-permute-start
  34.3 3.9 %collective-permute-done.1 = bf16[2,128,128]{2,1,0:T(8,128)(2,1)S(1)} collective-permute-done((bf16[2,128,128]{2,1,0:T(8,128)(2,1)S(1)}, bf16[2,128,128]{2,1,0:T(8,128)(2,1)S(1)}, u32[]{:S(2)}, u32[]{:S(2)}) %collective-permute-start.1) | collective-permute-done | bytes 65568 | tf_op jit(solution)/shard_map/ppermute | solution.py:330
  38.2 0.7 collective-permute-done
  39.0 1.5 %collective-permute-done.3.refs_5_ = bf16[8,128,128]{2,1,0:T(8,128)(2,1)S(1)} collective-permute-done((bf16[8,128,128]{2,1,0:T(8,128)(2,1)S(1)}, bf16[8,128,128]{2,1,0:T(8,128)(2,1)S(1)}, u32[]{:S(2)}, u32[]{:S(2)}) %collective-permute-start.3) | collective-permute-done | bytes 262176 | tf_op jit(solution)/shard_map/ppermute | solution.py:333
  40.5 3.6 %products.1 = (f32[32,128,128]{2,1,0:T(8,128)}, s16[2064,128]{1,0:T(8,128)(2,1)}, s16[2064,128]{1,0:T(8,128)(2,1)}) custom-call(s32[64]{0:T(128)S(1)} %copy-done.1, s32[64]{0:T(128)S(1)} %copy-done.2, s32[64]{0:T(128)S(1)} %copy-done.3, bf16[64,128,128]{2,1,0:T(8,128)(2,1)S(1)} %stage.1.refs_3_.refs_1_, bf16[8,128,128]{2,1,0:T(8,128)(2,1)S(1)} %pad_maximum_fusion.refs_4_, ...), custom_call_target="tpu_custom_call" | custom-call | tf_op jit(solution)/shard_map/products/pallas_call | solution.py:372
  44.1 0.6 collective-permute-start.4
  44.8 2.4 %collective-permute-start.5 = (s16[2064,128]{1,0:T(8,128)(2,1)}, s16[2064,128]{1,0:T(8,128)(2,1)S(1)}, u32[]{:S(2)}, u32[]{:S(2)}) collective-permute-start(s16[2064,128]{1,0:T(8,128)(2,1)} %get-tuple-element.24), channel_id=1, source_target_pairs={{0,7},{1,2},{2,1},{3,4},{4,3},{5,6},{6,5},{7,0},{8,15},{9,10},{10,... | collective-permute-start | bytes 1585160 | tf_op jit(solution)/shard_map/ppermute | solution.py:391
  47.2 38.3 %collective-permute-done.4.refs_1_ = s16[2064,128]{1,0:T(8,128)(2,1)S(1)} collective-permute-done((s16[2064,128]{1,0:T(8,128)(2,1)}, s16[2064,128]{1,0:T(8,128)(2,1)S(1)}, u32[]{:S(2)}, u32[]{:S(2)}) %collective-permute-start.4) | collective-permute-done | bytes 528416 | tf_op jit(solution)/shard_map/ppermute | solution.py:391
  85.4 1.0 collective-permute-done.5.refs_2_
  86.4 1.6 %copy-done = f32[32,128,128]{2,1,0:T(8,128)S(1)} copy-done((f32[32,128,128]{2,1,0:T(8,128)S(1)}, f32[32,128,128]{2,1,0:T(8,128)}, u32[]{:S(2)}) %copy-start) | copy-done | bytes 2097176
  88.4 1.6 %collective-permute-start.6 = (s16[1032,128]{1,0:T(8,128)(2,1)S(1)}, s16[1032,128]{1,0:T(8,128)(2,1)S(1)}, u32[]{:S(2)}, u32[]{:S(2)}) collective-permute-start(s16[1032,128]{1,0:T(8,128)(2,1)S(1)} %get-tuple-element.26), channel_id=1, source_target_pairs={{0,8},{8,16},{16,24},{24,0},{1,9},{9,17},{17,25},{25,1},{2,10},{10... | collective-permute-start | bytes 792584 | tf_op jit(solution)/shard_map/ppermute | solution.py:35
  90.6 5.3 %collective-permute-done.6.refs_1_ = s16[1032,128]{1,0:T(8,128)(2,1)S(1)} collective-permute-done((s16[1032,128]{1,0:T(8,128)(2,1)S(1)}, s16[1032,128]{1,0:T(8,128)(2,1)S(1)}, u32[]{:S(2)}, u32[]{:S(2)}) %collective-permute-start.6) | collective-permute-done | bytes 264224 | tf_op jit(solution)/shard_map/ppermute | solution.py:35
  95.9 1.2 %collective-permute-done.7.refs_2_ = s16[1032,128]{1,0:T(8,128)(2,1)S(1)} collective-permute-done((s16[1032,128]{1,0:T(8,128)(2,1)S(1)}, s16[1032,128]{1,0:T(8,128)(2,1)S(1)}, u32[]{:S(2)}, u32[]{:S(2)}) %collective-permute-start.7) | collective-permute-done | bytes 264224 | tf_op jit(solution)/shard_map/ppermute | solution.py:35
  97.3 1.3 %collective-permute-start.8 = (s16[520,128]{1,0:T(8,128)(2,1)S(1)}, s16[520,128]{1,0:T(8,128)(2,1)S(1)}, u32[]{:S(2)}, u32[]{:S(2)}) collective-permute-start(s16[520,128]{1,0:T(8,128)(2,1)S(1)} %get-tuple-element.29), channel_id=1, source_target_pairs={{0,8},{8,16},{16,24},{24,0},{1,9},{9,17},{17,25},{25,1},{2,10},{10... | collective-permute-start | bytes 399368 | tf_op jit(solution)/shard_map/ppermute | solution.py:35
  98.6 0.8 collective-permute-start.9
  99.4 3.0 %collective-permute-done.8.refs_3_ = s16[520,128]{1,0:T(8,128)(2,1)S(1)} collective-permute-done((s16[520,128]{1,0:T(8,128)(2,1)S(1)}, s16[520,128]{1,0:T(8,128)(2,1)S(1)}, u32[]{:S(2)}, u32[]{:S(2)}) %collective-permute-start.8) | collective-permute-done | bytes 133152 | tf_op jit(solution)/shard_map/ppermute | solution.py:35
  102.4 1.2 %collective-permute-done.9.refs_4_ = s16[520,128]{1,0:T(8,128)(2,1)S(1)} collective-permute-done((s16[520,128]{1,0:T(8,128)(2,1)S(1)}, s16[520,128]{1,0:T(8,128)(2,1)S(1)}, u32[]{:S(2)}, u32[]{:S(2)}) %collective-permute-start.9) | collective-permute-done | bytes 133152 | tf_op jit(solution)/shard_map/ppermute | solution.py:35
  103.9 3.5 %collective-permute-start.10 = (s16[264,128]{1,0:T(8,128)(2,1)S(1)}, s16[264,128]{1,0:T(8,128)(2,1)S(1)}, u32[]{:S(2)}, u32[]{:S(2)}) collective-permute-start(s16[264,128]{1,0:T(8,128)(2,1)S(1)} %get-tuple-element.32), channel_id=1, source_target_pairs={{0,2},{1,3},{2,4},{3,5},{4,6},{5,7},{6,0},{7,1},{8,10},{9,11},{10,... | collective-permute-start | bytes 202760 | tf_op jit(solution)/shard_map/ppermute | solution.py:35
  107.3 1.2 %collective-permute-start.11 = (s16[264,128]{1,0:T(8,128)(2,1)S(1)}, s16[264,128]{1,0:T(8,128)(2,1)S(1)}, u32[]{:S(2)}, u32[]{:S(2)}) collective-permute-start(s16[264,128]{1,0:T(8,128)(2,1)S(1)} %get-tuple-element.33), channel_id=1, source_target_pairs={{0,4},{1,5},{2,6},{3,7},{4,0},{5,1},{6,2},{7,3},{8,12},{9,13},{10,... | collective-permute-start | bytes 202760 | tf_op jit(solution)/shard_map/ppermute | solution.py:35
  108.5 4.0 %collective-permute-start.12 = (s16[264,128]{1,0:T(8,128)(2,1)S(1)}, s16[264,128]{1,0:T(8,128)(2,1)S(1)}, u32[]{:S(2)}, u32[]{:S(2)}) collective-permute-start(s16[264,128]{1,0:T(8,128)(2,1)S(1)} %get-tuple-element.34), channel_id=1, source_target_pairs={{0,6},{1,7},{2,0},{3,1},{4,2},{5,3},{6,4},{7,5},{8,14},{9,15},{10,... | collective-permute-start | bytes 202760 | tf_op jit(solution)/shard_map/ppermute | solution.py:35
  112.6 2.8 %list.1 = (s32[32]{0:T(128)}, s32[32]{0:T(128)}, s32[32]{0:T(128)}, s32[32]{0:T(128)S(1)}) custom-call(s32[32,2,128]{2,1,0:T(2,128)S(1)} %all-to-all-done.refs_0_), custom_call_target="tpu_custom_call" | custom-call | tf_op jit(solution)/shard_map/list/pallas_call | solution.py:353
  115.4 0.5 collective-permute-done.11.refs_2_
  115.9 0.7 last.1
  116.6 2.6 %keep.1 = bf16[32,128,128]{2,1,0:T(8,128)(2,1)} custom-call(s32[32]{0:T(128)S(1)} %get-tuple-element.35.refs_0_, bf16[64,128,128]{2,1,0:T(8,128)(2,1)} %all-to-all-done.1.refs_1_), custom_call_target="tpu_custom_call" | custom-call | tf_op jit(solution)/shard_map/keep/pallas_call | solution.py:434
  (19 shorter events, 1.8 us)
Async XLA Ops:
  2.1 19.2 %all-to-all-start = ((s32[32,2,128]{2,1,0:T(2,128)}), s32[32,2,128]{2,1,0:T(2,128)S(1)}, u32[]{:S(2)}, u32[]{:S(2)}) async-start(s32[32,2,128]{2,1,0:T(2,128)} %tell.1), calls=%async_computation | async-start | bytes 65536 | tf_op jit(solution)/shard_map/all_to_all | solution.py:331
  22.8 6.8 %copy-start.4 = (bf16[256,128]{1,0:T(8,128)(2,1)S(1)}, bf16[256,128]{1,0:T(8,128)(2,1)}, u32[]{:S(2)}) copy-start(bf16[256,128]{1,0:T(8,128)(2,1)} %param.5) | copy-start | bytes 196612
  22.8 17.8 %copy-start.1 = (s32[64]{0:T(128)S(1)}, s32[64]{0:T(128)}, u32[]{:S(2)}) copy-start(s32[64]{0:T(128)} %refs_0_.3) | copy-start | bytes 772
  22.8 17.8 %copy-start.2 = (s32[64]{0:T(128)S(1)}, s32[64]{0:T(128)}, u32[]{:S(2)}) copy-start(s32[64]{0:T(128)} %refs_1_.3) | copy-start | bytes 772
  22.8 17.7 %copy-start.3 = (s32[64]{0:T(128)S(1)}, s32[64]{0:T(128)}, u32[]{:S(2)}) copy-start(s32[64]{0:T(128)} %refs_2_.3) | copy-start | bytes 772
  22.8 93.8 %all-to-all-start.1 = ((bf16[64,128,128]{2,1,0:T(8,128)(2,1)}), bf16[64,128,128]{2,1,0:T(8,128)(2,1)}, u32[]{:S(2)}, u32[]{:S(2)}) async-start(bf16[64,128,128]{2,1,0:T(8,128)(2,1)} %plan.1), calls=%async_computation.1 | async-start | bytes 4194304 | tf_op jit(solution)/shard_map/all_to_all | solution.py:361
  29.6 4.7 %collective-permute-start.2 = (bf16[2,128,128]{2,1,0:T(8,128)(2,1)S(1)}, bf16[2,128,128]{2,1,0:T(8,128)(2,1)S(1)}, u32[]{:S(2)}, u32[]{:S(2)}) collective-permute-start(bf16[2,128,128]{2,1,0:T(8,128)(2,1)S(1)} %bitcast.1), channel_id=1, source_target_pairs={{0,192},{32,224},{64,0},{96,32},{128,64},{160,96},{192,128},{224,1... | collective-permute-start | bytes 196616 | tf_op jit(solution)/shard_map/ppermute | solution.py:330
  32.4 5.8 %collective-permute-start.1 = (bf16[2,128,128]{2,1,0:T(8,128)(2,1)S(1)}, bf16[2,128,128]{2,1,0:T(8,128)(2,1)S(1)}, u32[]{:S(2)}, u32[]{:S(2)}) collective-permute-start(bf16[2,128,128]{2,1,0:T(8,128)(2,1)S(1)} %bitcast.2), channel_id=1, source_target_pairs={{0,128},{32,160},{64,192},{96,224},{128,0},{160,32},{192,64},{224,... | collective-permute-start | bytes 196616 | tf_op jit(solution)/shard_map/ppermute | solution.py:330
  33.2 5.7 %collective-permute-start = (bf16[2,128,128]{2,1,0:T(8,128)(2,1)S(1)}, bf16[2,128,128]{2,1,0:T(8,128)(2,1)S(1)}, u32[]{:S(2)}, u32[]{:S(2)}) collective-permute-start(bf16[2,128,128]{2,1,0:T(8,128)(2,1)S(1)} %bitcast.3), channel_id=1, source_target_pairs={{0,64},{32,96},{64,128},{96,160},{128,192},{160,224},{192,0},{224,... | collective-permute-start | bytes 196616 | tf_op jit(solution)/shard_map/ppermute | solution.py:330
  38.9 1.6 %collective-permute-start.3 = (bf16[8,128,128]{2,1,0:T(8,128)(2,1)S(1)}, bf16[8,128,128]{2,1,0:T(8,128)(2,1)S(1)}, u32[]{:S(2)}, u32[]{:S(2)}) collective-permute-start(bf16[8,128,128]{2,1,0:T(8,128)(2,1)S(1)} %pad_maximum_fusion.refs_4_), channel_id=1, source_target_pairs={{0,32},{32,0},{64,96},{96,64},{128,160},{160,128},{192,224},{224,1... | collective-permute-start | bytes 786440 | tf_op jit(solution)/shard_map/ppermute | solution.py:333
  44.1 41.3 %collective-permute-start.4 = (s16[2064,128]{1,0:T(8,128)(2,1)}, s16[2064,128]{1,0:T(8,128)(2,1)S(1)}, u32[]{:S(2)}, u32[]{:S(2)}) collective-permute-start(s16[2064,128]{1,0:T(8,128)(2,1)} %get-tuple-element.23), channel_id=1, source_target_pairs={{0,1},{1,0},{2,3},{3,2},{4,5},{5,4},{6,7},{7,6},{8,9},{9,8},{10,11... | collective-permute-start | bytes 1585160 | tf_op jit(solution)/shard_map/ppermute | solution.py:391
  44.8 41.6 %collective-permute-start.5 = (s16[2064,128]{1,0:T(8,128)(2,1)}, s16[2064,128]{1,0:T(8,128)(2,1)S(1)}, u32[]{:S(2)}, u32[]{:S(2)}) collective-permute-start(s16[2064,128]{1,0:T(8,128)(2,1)} %get-tuple-element.24), channel_id=1, source_target_pairs={{0,7},{1,2},{2,1},{3,4},{4,3},{5,6},{6,5},{7,0},{8,15},{9,10},{10,... | collective-permute-start | bytes 1585160 | tf_op jit(solution)/shard_map/ppermute | solution.py:391
  86.4 1.6 %copy-start = (f32[32,128,128]{2,1,0:T(8,128)S(1)}, f32[32,128,128]{2,1,0:T(8,128)}, u32[]{:S(2)}) copy-start(f32[32,128,128]{2,1,0:T(8,128)} %get-tuple-element.22.refs_0_) | copy-start | bytes 6291460
  88.4 7.4 %collective-permute-start.6 = (s16[1032,128]{1,0:T(8,128)(2,1)S(1)}, s16[1032,128]{1,0:T(8,128)(2,1)S(1)}, u32[]{:S(2)}, u32[]{:S(2)}) collective-permute-start(s16[1032,128]{1,0:T(8,128)(2,1)S(1)} %get-tuple-element.26), channel_id=1, source_target_pairs={{0,8},{8,16},{16,24},{24,0},{1,9},{9,17},{17,25},{25,1},{2,10},{10... | collective-permute-start | bytes 792584 | tf_op jit(solution)/shard_map/ppermute | solution.py:35
  90.0 7.1 %collective-permute-start.7 = (s16[1032,128]{1,0:T(8,128)(2,1)S(1)}, s16[1032,128]{1,0:T(8,128)(2,1)S(1)}, u32[]{:S(2)}, u32[]{:S(2)}) collective-permute-start(s16[1032,128]{1,0:T(8,128)(2,1)S(1)} %get-tuple-element.27), channel_id=1, source_target_pairs={{0,24},{8,0},{16,8},{24,16},{1,25},{9,1},{17,9},{25,17},{2,26},{10... | collective-permute-start | bytes 792584 | tf_op jit(solution)/shard_map/ppermute | solution.py:35
  97.3 5.1 %collective-permute-start.8 = (s16[520,128]{1,0:T(8,128)(2,1)S(1)}, s16[520,128]{1,0:T(8,128)(2,1)S(1)}, u32[]{:S(2)}, u32[]{:S(2)}) collective-permute-start(s16[520,128]{1,0:T(8,128)(2,1)S(1)} %get-tuple-element.29), channel_id=1, source_target_pairs={{0,8},{8,16},{16,24},{24,0},{1,9},{9,17},{17,25},{25,1},{2,10},{10... | collective-permute-start | bytes 399368 | tf_op jit(solution)/shard_map/ppermute | solution.py:35
  98.6 5.0 %collective-permute-start.9 = (s16[520,128]{1,0:T(8,128)(2,1)S(1)}, s16[520,128]{1,0:T(8,128)(2,1)S(1)}, u32[]{:S(2)}, u32[]{:S(2)}) collective-permute-start(s16[520,128]{1,0:T(8,128)(2,1)S(1)} %get-tuple-element.30), channel_id=1, source_target_pairs={{0,24},{8,0},{16,8},{24,16},{1,25},{9,1},{17,9},{25,17},{2,26},{10... | collective-permute-start | bytes 399368 | tf_op jit(solution)/shard_map/ppermute | solution.py:35
  103.9 11.5 %collective-permute-start.10 = (s16[264,128]{1,0:T(8,128)(2,1)S(1)}, s16[264,128]{1,0:T(8,128)(2,1)S(1)}, u32[]{:S(2)}, u32[]{:S(2)}) collective-permute-start(s16[264,128]{1,0:T(8,128)(2,1)S(1)} %get-tuple-element.32), channel_id=1, source_target_pairs={{0,2},{1,3},{2,4},{3,5},{4,6},{5,7},{6,0},{7,1},{8,10},{9,11},{10,... | collective-permute-start | bytes 202760 | tf_op jit(solution)/shard_map/ppermute | solution.py:35
  107.3 8.6 %collective-permute-start.11 = (s16[264,128]{1,0:T(8,128)(2,1)S(1)}, s16[264,128]{1,0:T(8,128)(2,1)S(1)}, u32[]{:S(2)}, u32[]{:S(2)}) collective-permute-start(s16[264,128]{1,0:T(8,128)(2,1)S(1)} %get-tuple-element.33), channel_id=1, source_target_pairs={{0,4},{1,5},{2,6},{3,7},{4,0},{5,1},{6,2},{7,3},{8,12},{9,13},{10,... | collective-permute-start | bytes 202760 | tf_op jit(solution)/shard_map/ppermute | solution.py:35
  108.5 7.4 %collective-permute-start.12 = (s16[264,128]{1,0:T(8,128)(2,1)S(1)}, s16[264,128]{1,0:T(8,128)(2,1)S(1)}, u32[]{:S(2)}, u32[]{:S(2)}) collective-permute-start(s16[264,128]{1,0:T(8,128)(2,1)S(1)} %get-tuple-element.34), channel_id=1, source_target_pairs={{0,6},{1,7},{2,0},{3,1},{4,2},{5,3},{6,4},{7,5},{8,14},{9,15},{10,... | collective-permute-start | bytes 202760 | tf_op jit(solution)/shard_map/ppermute | solution.py:35
